TPU v7x, 16 devices: a 4x2x1 block of a 4x4x8 slice. The times are simulated.
16 devices in a mesh: dp: 2 (over y, z), sp: 8 (over x, core).
Axes of the slice: x: 4, y: 2, z: 1, core: 2. Of those that a mesh axis runs over, the one named last changes fastest.
The devices are a block of a 4x4x8 slice.
Arguments:
- tokens: bfloat16 [12, 4096, 2048], P('dp', 'sp'), parts along dimension 0
- w_query: bfloat16 [2048, 4096], replicated
- w_key: bfloat16 [2048, 512], replicated
- w_value: bfloat16 [2048, 512], replicated
- w_out: bfloat16 [4096, 2048], replicated
- attn_norm: bfloat16 [2048], replicated
- q_norm: bfloat16 [128], replicated
- k_norm: bfloat16 [128], replicated
Outputs:
- output 1: bfloat16 [12, 4096, 2048], P('dp', 'sp'), parts along dimension 0
- output 2: bfloat16 [12, 4096, 4, 128], P('dp', 'sp'), parts along dimension 0
- output 3: bfloat16 [12, 4096, 4, 128], P('dp', 'sp'), parts along dimension 0
There are 2 independent parts. A program takes and returns all parts, laid end to end along the dimension named above; an argument that names none is the same for every part.
All inputs are finite; a program needn't handle non-finite values.
Results may differ from a plain program's by a relative error of at most 0.00827115.
Values are sent between devices in bfloat16 or wider.
A program may use at most 768 MiB of HBM per device.

v0:
```python
import jax
import jax.numpy as jnp
from jax import lax
from jax.sharding import PartitionSpec as P

EPS = 1e-6
THETA = 1000000.0
HEAD_DIM = 128


def rms_norm(values, gain_vec):
    wide_vals = values.astype(jnp.float32)
    inv_rms = lax.rsqrt(jnp.mean(wide_vals * wide_vals, axis=-1, keepdims=True) + EPS)
    return wide_vals * inv_rms * gain_vec.astype(jnp.float32)


def rope_rotate(values, positions):
    half_dim = HEAD_DIM // 2
    inv_freq = THETA ** (-jnp.arange(half_dim, dtype=jnp.float32) * 2.0 / HEAD_DIM)
    angles = positions.astype(jnp.float32)[:, None] * inv_freq[None, :]
    cos_t = jnp.cos(angles)[None, :, None, :]
    sin_t = jnp.sin(angles)[None, :, None, :]
    lo_half = values[..., :half_dim]
    hi_half = values[..., half_dim:]
    return jnp.concatenate([lo_half * cos_t - hi_half * sin_t, hi_half * cos_t + lo_half * sin_t], axis=-1)


def qkv_local(tokens, w_query, w_key, w_value, attn_norm, q_norm, k_norm, positions):
    n_batch, n_tok, d_model = tokens.shape
    hidden = rms_norm(tokens, attn_norm).astype(jnp.bfloat16).reshape(n_batch * n_tok, d_model)

    def project(weight):
        flat_out = jnp.dot(hidden, weight, preferred_element_type=jnp.float32).astype(jnp.bfloat16)
        return flat_out.reshape(n_batch, n_tok, weight.shape[1] // HEAD_DIM, HEAD_DIM)

    q_rot = rope_rotate(rms_norm(project(w_query), q_norm), positions).astype(jnp.bfloat16)
    k_rot = rope_rotate(rms_norm(project(w_key), k_norm), positions).astype(jnp.bfloat16)
    return q_rot, k_rot, project(w_value)


def finish_block(tokens, attn_heads, w_out):
    n_batch, n_tok, d_model = tokens.shape
    flat_in = attn_heads.reshape(n_batch * n_tok, w_out.shape[0])
    proj_out = jnp.dot(flat_in, w_out, preferred_element_type=jnp.float32).reshape(n_batch, n_tok, d_model)
    return (tokens.astype(jnp.float32) + proj_out).astype(jnp.bfloat16)


def causal_attention(q_group, k_seq, v_seq, q_offset):
    n_batch, q_len, n_kv, n_group, head_dim = q_group.shape
    blk_len = min(256, q_len)
    n_qblk = q_len // blk_len
    scale = head_dim ** -0.5
    q_blocks = q_group.reshape(n_batch, n_qblk, blk_len, n_kv, n_group, head_dim)
    row_ids = jnp.arange(blk_len)
    stat_shape = (n_batch, blk_len, n_kv, n_group)

    def one_block(blk_idx):
        q_blk = lax.dynamic_index_in_dim(q_blocks, blk_idx, axis=1, keepdims=False)
        q_start = q_offset + blk_idx * blk_len
        n_kblk = q_start // blk_len + 1

        def key_step(key_blk, carry):
            run_max, run_sum, out_acc = carry
            k_blk = lax.dynamic_slice_in_dim(k_seq, key_blk * blk_len, blk_len, axis=1)
            v_blk = lax.dynamic_slice_in_dim(v_seq, key_blk * blk_len, blk_len, axis=1)
            scores = jnp.einsum('bqkgd,bskd->bqkgs', q_blk, k_blk, preferred_element_type=jnp.float32) * scale
            allowed = (key_blk * blk_len + row_ids)[None, :] <= (q_start + row_ids)[:, None]
            scores = jnp.where(allowed[None, :, None, None, :], scores, -jnp.inf)
            new_max = jnp.maximum(run_max, jnp.max(scores, axis=-1))
            rescale = jnp.exp(run_max - new_max)
            probs_blk = jnp.exp(scores - new_max[..., None])
            run_sum = run_sum * rescale + jnp.sum(probs_blk, axis=-1)
            out_acc = out_acc * rescale[..., None] + jnp.einsum('bqkgs,bskd->bqkgd', probs_blk.astype(jnp.bfloat16), v_blk, preferred_element_type=jnp.float32)
            return new_max, run_sum, out_acc

        init_state = (jnp.full(stat_shape, -jnp.inf, jnp.float32), jnp.zeros(stat_shape, jnp.float32), jnp.zeros(stat_shape + (head_dim,), jnp.float32))
        final_state = lax.fori_loop(0, n_kblk, key_step, init_state)
        return (final_state[2] / final_state[1][..., None]).astype(jnp.bfloat16)

    attn_blocks = lax.map(one_block, jnp.arange(n_qblk))
    return jnp.moveaxis(attn_blocks, 0, 1).reshape(n_batch, q_len, n_kv, n_group, head_dim)


def solution(mesh):
    n_sp = mesh.shape['sp']

    def per_device(tokens, w_query, w_key, w_value, w_out, attn_norm, q_norm, k_norm):
        n_batch, seq_loc, d_model = tokens.shape
        positions = lax.axis_index('sp') * seq_loc + jnp.arange(seq_loc)
        q_rot, k_rot, v_proj = qkv_local(tokens, w_query, w_key, w_value, attn_norm, q_norm, k_norm, positions)
        n_kv = k_rot.shape[2]
        copies = max(1, n_sp // n_kv)
        k_send = jnp.repeat(k_rot, copies, axis=2) if copies > 1 else k_rot
        v_send = jnp.repeat(v_proj, copies, axis=2) if copies > 1 else v_proj
        q_heads = lax.all_to_all(q_rot, 'sp', 2, 1, tiled=True)
        k_heads = lax.all_to_all(k_send, 'sp', 2, 1, tiled=True)
        v_heads = lax.all_to_all(v_send, 'sp', 2, 1, tiled=True)
        seq_len = q_heads.shape[1]
        h_loc = q_heads.shape[2]
        kv_loc = k_heads.shape[2]
        attn_out = causal_attention(q_heads.reshape(n_batch, seq_len, kv_loc, h_loc // kv_loc, HEAD_DIM), k_heads, v_heads, 0)
        attn_seq = lax.all_to_all(attn_out.reshape(n_batch, seq_len, h_loc, HEAD_DIM), 'sp', 1, 2, tiled=True)
        return finish_block(tokens, attn_seq, w_out), k_rot, v_proj

    spec_tok = P('dp', 'sp', None)
    spec_cache = P('dp', 'sp', None, None)
    spec_mat = P(None, None)
    spec_vec = P(None)
    return jax.shard_map(per_device, mesh=mesh, in_specs=(spec_tok, spec_mat, spec_mat, spec_mat, spec_mat, spec_vec, spec_vec, spec_vec), out_specs=(spec_tok, spec_cache, spec_cache), check_vma=False)
```

profile of v0, /device:TPU:112, one launch (start us, length us, event | category | flops | bytes accessed | tf_op | source)
XLA Modules:
  0.0 2267.7 jit_solution(16128112002870224526)
XLA Ops:
  72.2 60.9 %convert_bitcast_fusion = f32[384,8,32,128]{3,1,2,0:T(8,128)} fusion(bf16[3072,2048]{1,0:T(8,128)(2,1)} %bitcast.143, bf16[2048,4096]{1,0:T(8,128)(2,1)} %param.13), kind=kOutput, calls=%fused_computation.36 | convolution fusion | flops 51564773376 | bytes 79691776 | tf_op jit(solution)/shard_map/dot_general | solution.py:33
  133.1 40.9 %copy.97 = f32[384,8,32,128]{3,2,1,0:T(8,128)} copy(f32[384,8,32,128]{3,1,2,0:T(8,128)} %convert_bitcast_fusion) | data formatting | bytes 100663296
  174.0 16.9 multiply_reduce_fusion
  192.5 13.1 convolution_convert_fusion
  224.2 34.1 %fusion.26 = f32[6,512,32,128]{3,1,0,2:T(8,128)} fusion(f32[6,512,32,128]{3,2,1,0:T(8,128)} %bitcast.131, f32[128]{0:T(128)S(1)} %convert_element_type.65, f32[6,512,32]{1,0,2:T(8,128)S(1)} %copy-done.9), kind=kLoop, calls=%fused_computation.35 | loop fusion | flops 25165824 | bytes 101057024 | tf_op jit(solution)/shard_map/mul | solution.py:14
  258.3 49.8 %subtract_convert_fusion = (bf16[6,512,32,64]{3,1,0,2:T(8,128)(2,1)}, bf16[6,512,32,64]{3,1,0,2:T(8,128)(2,1)}) fusion(f32[6,512,32,128]{3,1,0,2:T(8,128)} %fusion.26, f32[512,64]{1,0:T(8,128)S(1)} %copy-done.8, f32[512,64]{1,0:T(8,128)S(1)} %copy-done.6), kind=kLoop, calls=%fused_computation.38 | loop fusion | flops 50331648 | bytes 75759616 | tf_op jit(solution)/shard_map/convert.4
  308.1 30.6 %pad_maximum_fusion = bf16[6,512,32,128]{3,1,0,2:T(8,128)(2,1)} fusion(bf16[6,512,32,64]{3,1,0,2:T(8,128)(2,1)} %get-tuple-element.290, bf16[6,512,32,64]{3,1,0,2:T(8,128)(2,1)} %get-tuple-element.289), kind=kLoop, calls=%fused_computation.47 | loop fusion | flops 50331648 | bytes 50331648 | tf_op jit(solution)/shard_map/concatenate | solution.py:25
  354.2 8.7 copy.85
  369.0 250.6 %all-to-all-done = bf16[6,512,32,128]{3,1,0,2:T(8,128)(2,1)} async-done(((bf16[6,512,32,128]{3,1,0,2:T(8,128)(2,1)}), bf16[6,512,32,128]{3,1,0,2:T(8,128)(2,1)}, u32[]{:S(2)}, u32[]{:S(2)}) %all-to-all-start) | async-done | bytes 25165856 | tf_op jit(solution)/shard_map/all_to_all | solution.py:95
  619.7 20.8 copy.77
  640.5 1171.3 %while.44 = (s32[]{:T(128)}, bf16[16,6,256,1,4,128]{5,2,0,4,1,3:T(8,128)(2,1)}, s32[16]{0:T(128)S(1)}, bf16[6,16,256,1,4,128]{5,2,1,4,0,3:T(8,128)(2,1)}, bf16[6...) while((s32[]{:T(128)}, ...), condition=%wide.region_8.9_spmd.clone.clone, body=%wide.region_3.8_spmd.clone.clone.sunk | while | flops 825838080 | bytes 45563092 | solution.py:80
  664.6 14.7 while.45
  690.1 22.0 while.45
  723.0 29.4 %while.45 = (s32[]{:T(128)}, f32[6,256,1,4]{1,3,0,2:T(4,128)S(1)}, f32[6,256,1,4]{1,3,0,2:T(4,128)S(1)}, f32[6,256,1,4,128]{1,4,3,0,2:T(8,128)S(1)}, s32[]{:T(12...) while((s32[]{:T(128)}, f32[6,256,1,4]{1,3,0,2:T(4,128)S(1)}, ...), condition=%wide.region_7.7_spmd.clone, body=%wide.region_4.6_spmd.clone.sunk | while | flops 824265216 | bytes 28185796 | solution.py:77
  763.1 36.7 %while.45 = (s32[]{:T(128)}, f32[6,256,1,4]{1,3,0,2:T(4,128)S(1)}, f32[6,256,1,4]{1,3,0,2:T(4,128)S(1)}, f32[6,256,1,4,128]{1,4,3,0,2:T(8,128)S(1)}, s32[]{:T(12...) while((s32[]{:T(128)}, f32[6,256,1,4]{1,3,0,2:T(4,128)S(1)}, ...), condition=%wide.region_7.7_spmd.clone, body=%wide.region_4.6_spmd.clone.sunk | while | flops 824265216 | bytes 28185796 | solution.py:77
  810.7 44.0 %while.45 = (s32[]{:T(128)}, f32[6,256,1,4]{1,3,0,2:T(4,128)S(1)}, f32[6,256,1,4]{1,3,0,2:T(4,128)S(1)}, f32[6,256,1,4,128]{1,4,3,0,2:T(8,128)S(1)}, s32[]{:T(12...) while((s32[]{:T(128)}, f32[6,256,1,4]{1,3,0,2:T(4,128)S(1)}, ...), condition=%wide.region_7.7_spmd.clone, body=%wide.region_4.6_spmd.clone.sunk | while | flops 824265216 | bytes 28185796 | solution.py:77
  865.5 51.4 %while.45 = (s32[]{:T(128)}, f32[6,256,1,4]{1,3,0,2:T(4,128)S(1)}, f32[6,256,1,4]{1,3,0,2:T(4,128)S(1)}, f32[6,256,1,4,128]{1,4,3,0,2:T(8,128)S(1)}, s32[]{:T(12...) while((s32[]{:T(128)}, f32[6,256,1,4]{1,3,0,2:T(4,128)S(1)}, ...), condition=%wide.region_7.7_spmd.clone, body=%wide.region_4.6_spmd.clone.sunk | while | flops 824265216 | bytes 28185796 | solution.py:77
  927.7 58.7 %while.45 = (s32[]{:T(128)}, f32[6,256,1,4]{1,3,0,2:T(4,128)S(1)}, f32[6,256,1,4]{1,3,0,2:T(4,128)S(1)}, f32[6,256,1,4,128]{1,4,3,0,2:T(8,128)S(1)}, s32[]{:T(12...) while((s32[]{:T(128)}, f32[6,256,1,4]{1,3,0,2:T(4,128)S(1)}, ...), condition=%wide.region_7.7_spmd.clone, body=%wide.region_4.6_spmd.clone.sunk | while | flops 824265216 | bytes 28185796 | solution.py:77
  997.2 66.1 %while.45 = (s32[]{:T(128)}, f32[6,256,1,4]{1,3,0,2:T(4,128)S(1)}, f32[6,256,1,4]{1,3,0,2:T(4,128)S(1)}, f32[6,256,1,4,128]{1,4,3,0,2:T(8,128)S(1)}, s32[]{:T(12...) while((s32[]{:T(128)}, f32[6,256,1,4]{1,3,0,2:T(4,128)S(1)}, ...), condition=%wide.region_7.7_spmd.clone, body=%wide.region_4.6_spmd.clone.sunk | while | flops 824265216 | bytes 28185796 | solution.py:77
  1074.1 73.4 %while.45 = (s32[]{:T(128)}, f32[6,256,1,4]{1,3,0,2:T(4,128)S(1)}, f32[6,256,1,4]{1,3,0,2:T(4,128)S(1)}, f32[6,256,1,4,128]{1,4,3,0,2:T(8,128)S(1)}, s32[]{:T(12...) while((s32[]{:T(128)}, f32[6,256,1,4]{1,3,0,2:T(4,128)S(1)}, ...), condition=%wide.region_7.7_spmd.clone, body=%wide.region_4.6_spmd.clone.sunk | while | flops 824265216 | bytes 28185796 | solution.py:77
  1158.3 80.7 %while.45 = (s32[]{:T(128)}, f32[6,256,1,4]{1,3,0,2:T(4,128)S(1)}, f32[6,256,1,4]{1,3,0,2:T(4,128)S(1)}, f32[6,256,1,4,128]{1,4,3,0,2:T(8,128)S(1)}, s32[]{:T(12...) while((s32[]{:T(128)}, f32[6,256,1,4]{1,3,0,2:T(4,128)S(1)}, ...), condition=%wide.region_7.7_spmd.clone, body=%wide.region_4.6_spmd.clone.sunk | while | flops 824265216 | bytes 28185796 | solution.py:77
  1249.9 88.1 %while.45 = (s32[]{:T(128)}, f32[6,256,1,4]{1,3,0,2:T(4,128)S(1)}, f32[6,256,1,4]{1,3,0,2:T(4,128)S(1)}, f32[6,256,1,4,128]{1,4,3,0,2:T(8,128)S(1)}, s32[]{:T(12...) while((s32[]{:T(128)}, f32[6,256,1,4]{1,3,0,2:T(4,128)S(1)}, ...), condition=%wide.region_7.7_spmd.clone, body=%wide.region_4.6_spmd.clone.sunk | while | flops 824265216 | bytes 28185796 | solution.py:77
  1348.8 95.4 %while.45 = (s32[]{:T(128)}, f32[6,256,1,4]{1,3,0,2:T(4,128)S(1)}, f32[6,256,1,4]{1,3,0,2:T(4,128)S(1)}, f32[6,256,1,4,128]{1,4,3,0,2:T(8,128)S(1)}, s32[]{:T(12...) while((s32[]{:T(128)}, f32[6,256,1,4]{1,3,0,2:T(4,128)S(1)}, ...), condition=%wide.region_7.7_spmd.clone, body=%wide.region_4.6_spmd.clone.sunk | while | flops 824265216 | bytes 28185796 | solution.py:77
  1455.0 102.7 %while.45 = (s32[]{:T(128)}, f32[6,256,1,4]{1,3,0,2:T(4,128)S(1)}, f32[6,256,1,4]{1,3,0,2:T(4,128)S(1)}, f32[6,256,1,4,128]{1,4,3,0,2:T(8,128)S(1)}, s32[]{:T(12...) while((s32[]{:T(128)}, f32[6,256,1,4]{1,3,0,2:T(4,128)S(1)}, ...), condition=%wide.region_7.7_spmd.clone, body=%wide.region_4.6_spmd.clone.sunk | while | flops 824265216 | bytes 28185796 | solution.py:77
  1568.6 110.1 %while.45 = (s32[]{:T(128)}, f32[6,256,1,4]{1,3,0,2:T(4,128)S(1)}, f32[6,256,1,4]{1,3,0,2:T(4,128)S(1)}, f32[6,256,1,4,128]{1,4,3,0,2:T(8,128)S(1)}, s32[]{:T(12...) while((s32[]{:T(128)}, f32[6,256,1,4]{1,3,0,2:T(4,128)S(1)}, ...), condition=%wide.region_7.7_spmd.clone, body=%wide.region_4.6_spmd.clone.sunk | while | flops 824265216 | bytes 28185796 | solution.py:77
  1689.5 117.4 %while.45 = (s32[]{:T(128)}, f32[6,256,1,4]{1,3,0,2:T(4,128)S(1)}, f32[6,256,1,4]{1,3,0,2:T(4,128)S(1)}, f32[6,256,1,4,128]{1,4,3,0,2:T(8,128)S(1)}, s32[]{:T(12...) while((s32[]{:T(128)}, f32[6,256,1,4]{1,3,0,2:T(4,128)S(1)}, ...), condition=%wide.region_7.7_spmd.clone, body=%wide.region_4.6_spmd.clone.sunk | while | flops 824265216 | bytes 28185796 | solution.py:77
  1811.8 32.3 %copy.87 = bf16[6,4096,4,128]{3,2,0,1:T(4,128)(2,1)} copy(bf16[6,4096,4,128]{3,1,2,0:T(8,128)(2,1)} %bitcast.138) | data formatting | bytes 50331648 | tf_op jit(solution)/shard_map/reshape;reshape | solution.py:102
  1844.0 279.1 %all_to_all.66 = bf16[6,4096,4,128]{3,2,0,1:T(4,128)(2,1)S(1)} all-to-all(bf16[6,4096,4,128]{3,2,0,1:T(4,128)(2,1)} %copy.87), channel_id=1, replica_groups=mesh['dp'=2,'sp'=8] {'sp'}, dimensions={1} | all-to-all | bytes 50331648 | tf_op jit(solution)/shard_map/all_to_all | solution.py:102
  2123.1 8.9 copy.88
  2132.0 32.2 %copy.89 = bf16[6,512,8,4,128]{4,3,2,1,0:T(4,128)(2,1)} copy(bf16[6,512,8,4,128]{4,1,2,3,0:T(8,128)(2,1)} %bitcast.134) | data formatting | bytes 50331648 | tf_op jit(solution)/shard_map/all_to_all | solution.py:102
  2164.3 41.0 %dot_general.25 = bf16[6,512,4096]{2,1,0:T(8,128)(2,1)} reshape(bf16[6,512,8,4,128]{4,3,2,1,0:T(4,128)(2,1)} %copy.89) | data formatting | bytes 50331648 | tf_op jit(solution)/shard_map/dot_general | solution.py:44
  2205.3 62.1 %fusion.30 = bf16[6,512,2048]{2,1,0:T(8,128)(2,1)} fusion(bf16[6,512,2048]{2,1,0:T(8,128)(2,1)} %param.12, bf16[6,512,4096]{2,1,0:T(8,128)(2,1)} %dot_general.25, bf16[4096,2048]{1,0:T(8,128)(2,1)} %param.16), kind=kOutput, calls=%fused_computation.46 | convolution fusion | flops 51558481920 | bytes 67108864 | tf_op jit(solution)/shard_map/dot_general | solution.py:44
  (1292 shorter events, 1243.1 us)
Async XLA Ops:
  0.6 19.8 copy-start
  0.7 7.3 copy-start.10
  15.7 4.8 copy-start.2
  36.7 6.4 copy-start.11
  51.3 4.3 copy-start.5
  51.3 4.3 copy-start.7
  60.5 1.7 copy-start.4
  66.9 146.9 %all-to-all-start.1 = ((bf16[6,512,8,128]{3,1,0,2:T(8,128)(2,1)}), bf16[6,512,8,128]{3,1,0,2:T(8,128)(2,1)}, u32[]{:S(2)}, u32[]{:S(2)}) async-start(bf16[6,512,8,128]{3,1,0,2:T(8,128)(2,1)} %bitcast.139), calls=%async_computation.1 | async-start | bytes 12582912 | tf_op jit(solution)/shard_map/all_to_all | solution.py:96
  174.0 18.5 copy-start.12
  209.4 9.6 copy-start.3
  219.1 5.1 copy-start.9
  219.1 119.6 %all-to-all-start.2 = ((bf16[6,512,8,128]{1,3,0,2:T(8,128)(2,1)}), bf16[6,512,8,128]{1,3,0,2:T(8,128)(2,1)}, u32[]{:S(2)}, u32[]{:S(2)}) async-start(bf16[6,512,8,128]{1,3,0,2:T(8,128)(2,1)} %bitcast.140), calls=%async_computation.2 | async-start | bytes 12582912 | tf_op jit(solution)/shard_map/all_to_all | solution.py:97
  224.2 34.1 %copy-start.6 = (f32[512,64]{1,0:T(8,128)S(1)}, f32[512,64]{1,0:T(8,128)}, u32[]{:S(2)}) copy-start(f32[512,64]{1,0:T(8,128)} %copy-done.5) | copy-start | bytes 393220
  224.2 34.1 %copy-start.8 = (f32[512,64]{1,0:T(8,128)S(1)}, f32[512,64]{1,0:T(8,128)}, u32[]{:S(2)}) copy-start(f32[512,64]{1,0:T(8,128)} %copy-done.7) | copy-start | bytes 393220
  338.7 281.0 %all-to-all-start = ((bf16[6,512,32,128]{3,1,0,2:T(8,128)(2,1)}), bf16[6,512,32,128]{3,1,0,2:T(8,128)(2,1)}, u32[]{:S(2)}, u32[]{:S(2)}) async-start(bf16[6,512,32,128]{3,1,0,2:T(8,128)(2,1)} %pad_maximum_fusion), calls=%async_computation | async-start | bytes 50331648 | tf_op jit(solution)/shard_map/all_to_all | solution.py:95
  2205.3 62.1 %copy-start.1 = (bf16[2048,512]{1,0:T(8,128)(2,1)S(1)}, bf16[2048,512]{1,0:T(8,128)(2,1)}, u32[]{:S(2)}) copy-start(bf16[2048,512]{1,0:T(8,128)(2,1)} %param.14) | copy-start | bytes 6291460
where the time goes:
time: 2280 us; the launch traced here: 2270 us
  matrix products  932 us (41%)
  other arithmetic  394 us (17%)
  local copies, waits for them, and re-layouts  345 us (15%)
  blocking collectives  279 us (12%)
  waiting for transfers between devices  251 us (11%)
  loops' own time  48.6 us (2%)
    dot_general x136, matrix products, key_step(): jnp.einsum('bqkgs,bskd->bqkgd', probs_blk.astype(jnp.bfloat16), v_blk, pr...  440 us
    dot_general x136, matrix products, key_step(): jnp.einsum('bqkgd,bskd->bqkgs', q_blk, k_blk, preferred_element_type=jnp....  347 us
    all_to_all x1, blocking collectives, per_device(): lax.all_to_all(attn_out.reshape(n_batch, seq_len, h_loc, HEAD_DIM), 'sp',...  279 us
    all_to_all x1, waiting for transfers between devices, per_device(): q_heads = lax.all_to_all(q_rot, 'sp', 2, 1, tiled=True)  251 us
    reduce_sum x136, other arithmetic, key_step(): run_sum = run_sum * rescale + jnp.sum(probs_blk, axis=-1)  179 us
    dot_general x3, matrix products, project(): jnp.dot(hidden, weight, preferred_element_type=jnp.float32)  82.7 us
    dot_general x1, matrix products, finish_block(): jnp.dot(flat_in, w_out, preferred_element_type=jnp.float32)  62.1 us
    unnamed x28, local copies, waits for them, and re-layouts  56.1 us
  transfers between devices with their start and end apart: 3, of which 1 were waited for; matrix products, arithmetic and copies ran while one was open for 12% of the time, Pallas kernels for 0%

commit v1 on v0

v1 whole, which is shorter than its diff:
```python
import functools
import math

import jax
import jax.numpy as jnp
import numpy as np
from jax import lax
from jax.experimental import pallas as pl
from jax.experimental.pallas import tpu as pltpu
from jax.sharding import PartitionSpec as P

EPS = 1e-6
THETA = 1000000.0
HD = 128
T = 64
VMEM_LIMIT = 60 * 1024 * 1024
Q_COLS = 512
DIAG_STEP = 256
TILE_COST, ITEM_COST = 15.0, 9.5


def split_work(n_sp, n_tiles):
    moved = [0] * n_sp
    for d in range((n_sp + 1) // 2, n_sp):
        low = n_sp - 1 - d
        heavy, light = TILE_COST + ITEM_COST * (d + 1), TILE_COST + ITEM_COST * (low + 1)
        moved[d] = min(range(n_tiles // 2 + 1), key=lambda k: max(n_tiles * heavy - k * heavy, n_tiles * light + k * heavy))
    return moved


def normed(x_ref, gain_ref):
    p, r, d = x_ref.shape
    x = x_ref[...].reshape(p * r, d).astype(jnp.float32)
    inv = lax.rsqrt(jnp.mean(x * x, axis=-1, keepdims=True) + EPS)
    return (x * inv * gain_ref[...].astype(jnp.float32)).astype(jnp.bfloat16)


def head_norm_rope(y, gain, cos, sin, n_rep):
    inv = lax.rsqrt(jnp.mean(y * y, axis=-1, keepdims=True) + EPS)
    y = y * inv * gain
    rolled = pltpu.roll(y, HD // 2, 1)
    r = cos.shape[0]
    y, rolled = y.reshape(n_rep, r, HD), rolled.reshape(n_rep, r, HD)
    return (y * cos[None] + rolled * sin[None]).astype(jnp.bfloat16)


def kv_kernel(x_ref, wk_ref, wv_ref, g_ref, kg_ref, cos_ref, sin_ref, k_ref, v_ref, pack_ref):
    n_p, r, _ = x_ref.shape
    i = pl.program_id(0)
    h = normed(x_ref, g_ref)
    k = jnp.dot(h, wk_ref[...], preferred_element_type=jnp.float32).astype(jnp.bfloat16).astype(jnp.float32)
    v = jnp.dot(h, wv_ref[...], preferred_element_type=jnp.float32).astype(jnp.bfloat16)
    gain = kg_ref[...].astype(jnp.float32)
    cos, sin = cos_ref[...], sin_ref[...]
    rows = pl.ds(pl.multiple_of(i * r, r), r)
    v_ref[...] = v.reshape(v_ref.shape)
    for p in range(n_p):
        pack_ref[p, 1, :, rows] = v[p * r:(p + 1) * r].T
    for j in range(k.shape[1] // HD):
        y = head_norm_rope(k[:, j * HD:(j + 1) * HD], gain, cos, sin, n_p)
        k_ref[:, :, j * HD:(j + 1) * HD] = y
        pack_ref[:, 0, rows, j * HD:(j + 1) * HD] = y


def kv_project(x, w_key, w_value, gain, k_gain, cos, sin):
    n_p, rows, d = x.shape
    w = w_key.shape[1]
    r = min(128, rows)
    whole = lambda shape: pl.BlockSpec(shape, lambda i: (0,) * len(shape))
    return pl.pallas_call(
        kv_kernel,
        out_shape=(
            jax.ShapeDtypeStruct((n_p, rows, w), x.dtype),
            jax.ShapeDtypeStruct((n_p, rows, w), x.dtype),
            jax.ShapeDtypeStruct((n_p, 2, rows, w), x.dtype),
        ),
        grid=(rows // r,),
        in_specs=[
            pl.BlockSpec((n_p, r, d), lambda i: (0, i, 0)),
            whole((d, w)), whole((d, w)), whole((1, d)), whole((1, HD)),
            pl.BlockSpec((r, HD), lambda i: (i, 0)), pl.BlockSpec((r, HD), lambda i: (i, 0)),
        ],
        out_specs=(
            pl.BlockSpec((n_p, r, w), lambda i: (0, i, 0)),
            pl.BlockSpec((n_p, r, w), lambda i: (0, i, 0)),
            whole((n_p, 2, rows, w)),
        ),
        compiler_params=pltpu.CompilerParams(dimension_semantics=("arbitrary",), vmem_limit_bytes=VMEM_LIMIT),
        cost_estimate=pl.CostEstimate(flops=4 * n_p * rows * d * w, bytes_accessed=8 * n_p * rows * d, transcendentals=0),
        name="kv_proj",
    )(x, w_key, w_value, gain, k_gain, cos, sin)


def q_kernel(first_tile, nc, valid_ref, x_ref, w_ref, g_ref, qg_ref, cos_ref, sin_ref, *rest):
    q_ref, h_scr, y_scr = rest[-3:]
    n_p, _, _ = x_ref.shape

    @pl.when(valid_ref[first_tile + pl.program_id(0)] == 1)
    def _():
        h_scr[...] = normed(x_ref, g_ref)
        gain = qg_ref[...].astype(jnp.float32) * (math.log2(math.e) / math.sqrt(HD))
        cos, sin = cos_ref[...], sin_ref[...]
        n_chunks = w_ref.shape[1] // nc

        def project(n):
            cols = pl.ds(pl.multiple_of(n * nc, nc), nc)
            y_scr[...] = jnp.dot(h_scr[...], w_ref[:, cols], preferred_element_type=jnp.float32).astype(jnp.bfloat16)

        def finish(n):
            for j in range(nc // HD):
                y = head_norm_rope(y_scr[:, j * HD:(j + 1) * HD].astype(jnp.float32), gain, cos, sin, n_p)
                q_ref[:, :, pl.ds(pl.multiple_of(n * nc + j * HD, HD), HD)] = y

        def step(n, _):
            finish(n)
            project(n + 1)
            return 0

        project(0)
        lax.fori_loop(0, n_chunks - 1, step, 0)
        finish(n_chunks - 1)


def q_project(x, w_query, gain, q_gain, cos, sin, valid, first_tile, total_tiles, into):
    n_p, rows, d = x.shape
    w = w_query.shape[1]
    whole = lambda shape: pl.BlockSpec(shape, lambda i, *_: (0,) * len(shape))
    args = [valid, x, w_query, gain, q_gain, cos, sin]
    specs = [
        pl.BlockSpec((n_p, T, d), lambda i, *_: (0, i, 0)),
        pl.BlockSpec((d, w), lambda i, *_: (0, 0), pipeline_mode=pl.Buffered(1)),
        whole((1, d)), whole((1, HD)),
        pl.BlockSpec((T, HD), lambda i, *_: (i + first_tile, 0)), pl.BlockSpec((T, HD), lambda i, *_: (i + first_tile, 0)),
    ]
    alias = {}
    if into is not None:
        args.append(into)
        specs.append(pl.BlockSpec(memory_space=pl.ANY))
        alias = {7: 0}
    return pl.pallas_call(
        functools.partial(q_kernel, first_tile, Q_COLS),
        out_shape=jax.ShapeDtypeStruct((n_p, total_tiles * T, w), x.dtype),
        grid_spec=pltpu.PrefetchScalarGridSpec(
            num_scalar_prefetch=1,
            grid=(rows // T,),
            in_specs=specs,
            out_specs=pl.BlockSpec((n_p, T, w), lambda i, *_: (0, i + first_tile, 0)),
            scratch_shapes=[pltpu.VMEM((n_p * T, d), x.dtype), pltpu.VMEM((n_p * T, Q_COLS), x.dtype)],
        ),
        input_output_aliases=alias,
        compiler_params=pltpu.CompilerParams(dimension_semantics=("arbitrary",), vmem_limit_bytes=VMEM_LIMIT),
        cost_estimate=pl.CostEstimate(flops=2 * n_p * rows * d * w, bytes_accessed=2 * n_p * rows * (d + w), transcendentals=0),
        name="q_proj",
    )(*args)


def attn_kernel(n_tiles, grp, bk, ext_step, hp, ck, info_ref, q_ref, k_ref, v_ref, after_ref, o_ref, q_scr, s_scr, bm_scr, m_scr, l_scr, acc_scr):
    del after_ref
    n = grp * T
    base = 2 * n_tiles + 2
    m_items = (info_ref.shape[0] - base) // 4

    def tile(i): return info_ref[base + i]

    def blk(i): return info_ref[base + m_items + i]

    def first(i): return info_ref[base + 2 * m_items + i]

    def diag(i): return info_ref[base + 3 * m_items + i]

    @pl.when((pl.program_id(0) == 0) & (pl.program_id(1) == 0))
    def _():
        l_scr[...] = jnp.zeros_like(l_scr)
        acc_scr[...] = jnp.zeros_like(acc_scr)
        m_scr[...] = jnp.zeros_like(m_scr)

    for h in range(hp):
        for t in range(n_tiles):
            for j in range(grp):
                q_scr[h, t, j * T:(j + 1) * T, :] = q_ref[0, t * T:(t + 1) * T, (h * grp + j) * HD:(h * grp + j + 1) * HD]

    def fold(x, op):
        return op(x.reshape(x.shape[0] // 8, 8, n), axis=0)

    def qk_chunk(i, h, r):
        s = lax.dot_general(k_ref[blk(i), r * ck:(r + 1) * ck, h * HD:(h + 1) * HD], q_scr[h, tile(i)], (((1,), (1,)), ((), ())), preferred_element_type=jnp.float32)
        s_scr[h, r * ck:(r + 1) * ck, :] = s
        return fold(s, jnp.max)

    def masked_chunk(i, h, r, ext):
        s = s_scr[h, r * ck:r * ck + ext, :]
        off = info_ref[n_tiles + tile(i)] - blk(i) * bk - r * ck
        row = lax.broadcasted_iota(jnp.int32, (ext, n), 0)
        col = lax.broadcasted_iota(jnp.int32, (ext, n), 1) & (T - 1)
        return jnp.where(row - col <= off, s, -jnp.inf)

    def body(i, ext, masked):
        b = blk(i)
        fresh = first(i) == 1
        for h in range(hp):
            if masked:
                bm = jnp.full((8, n), -jnp.inf, jnp.float32)
                for r in range(bk // ck):
                    e = min(ck, ext - r * ck)
                    if e <= 0:
                        continue
                    if r * ck + e > ext - ext_step:
                        sm = masked_chunk(i, h, r, e)
                        s_scr[h, r * ck:r * ck + e, :] = sm
                    else:
                        sm = s_scr[h, r * ck:r * ck + e, :]
                    bm = jnp.maximum(bm, fold(sm, jnp.max))
            else:
                bm = bm_scr[h]
            m_old = jnp.where(fresh, -jnp.inf, m_scr[h])
            m_new = jnp.maximum(m_old, jnp.max(bm, axis=0, keepdims=True))
            m_scr[h] = m_new
            alpha = jnp.exp2(m_old - m_new)
            l = l_scr[h] * alpha
            pv = None
            bm_next = None
            for r in range(bk // ck):
                e = min(ck, ext - r * ck)
                if e > 0:
                    p = jnp.exp2(s_scr[h, r * ck:r * ck + e, :] - m_new)
                    l = l + fold(p, jnp.sum)
                    d = jnp.dot(v_ref[b, h * HD:(h + 1) * HD, r * ck:r * ck + e], p.astype(jnp.bfloat16), preferred_element_type=jnp.float32)
                    pv = d if pv is None else pv + d
                x = qk_chunk(i + 1, h, r)
                bm_next = x if bm_next is None else jnp.maximum(bm_next, x)
            l_scr[h] = l
            bm_scr[h] = bm_next
            acc_scr[h] = acc_scr[h] * alpha + pv

    def finish(i):
        t = tile(i)
        for h in range(hp):
            inv = 1.0 / jnp.sum(l_scr[h], axis=0, keepdims=True)
            o = (acc_scr[h] * inv).T.astype(o_ref.dtype)
            for j in range(grp):
                o_ref[0, pl.ds(pl.multiple_of(t * T, T), T), (h * grp + j) * HD:(h * grp + j + 1) * HD] = o[j * T:(j + 1) * T]

    cnt = info_ref[2 * n_tiles]

    @pl.when(cnt > 0)
    def _():
        for h in range(hp):
            bm = None
            for r in range(bk // ck):
                x = qk_chunk(0, h, r)
                bm = x if bm is None else jnp.maximum(bm, x)
            bm_scr[h] = bm

        def step(i, _):
            d = diag(i)

            @pl.when(d == 0)
            def _():
                body(i, bk, False)

            for e in range(bk // ext_step):
                @pl.when(d == e + 1)
                def _():
                    body(i, (e + 1) * ext_step, True)
                    finish(i)
            return 0

        lax.fori_loop(0, cnt, step, 0)


def make_info(n_sp, seq_loc, moved, ext_step):
    n_tiles, spare = seq_loc // T, max(moved)
    rows = []
    for me in range(n_sp):
        other = n_sp - 1 - me
        pos = [me * seq_loc + t * T for t in range(n_tiles)]
        pos += [(other + 1) * seq_loc - (spare - t) * T for t in range(spare)]
        valid = [t < n_tiles - moved[me] for t in range(n_tiles)] + [t >= spare - moved[other] for t in range(spare)]
        items = []
        for t, p in enumerate(pos):
            if valid[t]:
                last = p // seq_loc
                for b in range(last + 1):
                    items.append((t, b, int(b == 0), (p - last * seq_loc) // ext_step + 1 if b == last else 0))
        rows.append(([int(v) for v in valid] + pos + [len(items), int(moved[other] > 0)], items))
    m = max(len(items) for _, items in rows) + 1
    out = []
    for head, items in rows:
        items = items + [(0, 0, 0, 0)] * (m - len(items))
        out.append(head + [item[k] for k in range(4) for item in items])
    return np.asarray(out, np.int32)


def attention(q, kv, info, after, first_prompt, n_kv, hp=4, ck=256):
    _, rows, width = q.shape
    grp = width // HD // n_kv
    n_dev, nb, _, bk, _ = kv.shape
    n_tiles = rows // T
    n = grp * T
    block = pl.BlockSpec((1, rows, hp * grp * HD), lambda p, h, *_: (p + first_prompt, 0, h))
    flops = 2 * 4 * nb * rows * width * n_dev * bk // 2
    return pl.pallas_call(
        functools.partial(attn_kernel, n_tiles, grp, bk, DIAG_STEP, hp, ck),
        out_shape=jax.ShapeDtypeStruct((nb, rows, width), q.dtype),
        grid_spec=pltpu.PrefetchScalarGridSpec(
            num_scalar_prefetch=1,
            grid=(nb, n_kv // hp),
            in_specs=[
                block,
                pl.BlockSpec((n_dev, None, None, bk, hp * HD), lambda p, h, *_: (0, p, 0, 0, h)),
                pl.BlockSpec((n_dev, None, None, hp * HD, bk), lambda p, h, *_: (0, p, 1, h, 0)),
                pl.BlockSpec(memory_space=pl.ANY),
            ],
            out_specs=pl.BlockSpec((1, rows, hp * grp * HD), lambda p, h, *_: (p, 0, h)),
            scratch_shapes=[
                pltpu.VMEM((hp, n_tiles, n, HD), q.dtype),
                pltpu.VMEM((hp, bk, n), jnp.float32),
                pltpu.VMEM((hp, 8, n), jnp.float32),
                pltpu.VMEM((hp, 1, n), jnp.float32),
                pltpu.VMEM((hp, 8, n), jnp.float32),
                pltpu.VMEM((hp, HD, n), jnp.float32),
            ],
        ),
        compiler_params=pltpu.CompilerParams(dimension_semantics=("arbitrary", "arbitrary"), vmem_limit_bytes=VMEM_LIMIT),
        cost_estimate=pl.CostEstimate(flops=flops, bytes_accessed=4 * nb * rows * width, transcendentals=0),
        name="attn",
    )(info, q, kv, kv, after)


def out_moved_kernel(flag, info_ref, o_ref, w_ref, x_ref, y_ref):
    @pl.when(info_ref[flag] == 1)
    def _():
        n_p, r, w = o_ref.shape
        y = jnp.dot(o_ref[...].reshape(n_p * r, w), w_ref[...], preferred_element_type=jnp.float32)
        y_ref[...] = (x_ref[...].astype(jnp.float32) + y.reshape(n_p, r, -1)).astype(y_ref.dtype)


def out_moved(o, w_out, x, info, first_prompt):
    nb, all_rows, w = o.shape
    _, rows, d = x.shape
    first = all_rows - rows
    nc = min(512, d)
    return pl.pallas_call(
        functools.partial(out_moved_kernel, 2 * all_rows // T + 1),
        out_shape=jax.ShapeDtypeStruct((nb, rows, d), x.dtype),
        grid_spec=pltpu.PrefetchScalarGridSpec(
            num_scalar_prefetch=1,
            grid=(d // nc,),
            in_specs=[
                pl.BlockSpec((pl.Element(nb), pl.Element(rows), pl.Element(w)), lambda i, *_: (0, first, 0)),
                pl.BlockSpec((w, nc), lambda i, *_: (0, i)),
                pl.BlockSpec((pl.Element(nb), pl.Element(rows), pl.Element(nc)), lambda i, *_: (first_prompt, 0, i * nc)),
            ],
            out_specs=pl.BlockSpec((nb, rows, nc), lambda i, *_: (0, 0, i)),
        ),
        compiler_params=pltpu.CompilerParams(dimension_semantics=("arbitrary",), vmem_limit_bytes=VMEM_LIMIT),
        cost_estimate=pl.CostEstimate(flops=2 * nb * rows * d * w, bytes_accessed=2 * w * d, transcendentals=0),
        name="out_moved",
    )(info, o, w_out, x)


def out_kernel(n_g, nc, valid_ref, *refs):
    o_refs, (w_ref, x_ref, y_ref, o_scr) = refs[:n_g], refs[n_g:]

    @pl.when(valid_ref[pl.program_id(0)] == 1)
    def _():
        n_p, r, _ = x_ref.shape
        at = 0
        for o_ref in o_refs:
            nb, _, w = o_ref.shape
            o_scr[at:at + nb * r, :] = o_ref[...].reshape(nb * r, w)
            at += nb * r

        def chunk(n, _):
            cols = pl.ds(pl.multiple_of(n * nc, nc), nc)
            y = jnp.dot(o_scr[...], w_ref[:, cols], preferred_element_type=jnp.float32)
            y_ref[:, :, cols] = (x_ref[:, :, cols].astype(jnp.float32) + y.reshape(n_p, r, nc)).astype(y_ref.dtype)
            return 0

        lax.fori_loop(0, w_ref.shape[1] // nc, chunk, 0)


def out_local(o_parts, w_out, x, valid):
    n_p, rows, d = x.shape
    w = o_parts[0].shape[2]
    n_g = len(o_parts)
    return pl.pallas_call(
        functools.partial(out_kernel, n_g, 512),
        out_shape=jax.ShapeDtypeStruct(x.shape, x.dtype),
        grid_spec=pltpu.PrefetchScalarGridSpec(
            num_scalar_prefetch=1,
            grid=(rows // T,),
            in_specs=[pl.BlockSpec((o.shape[0], T, w), lambda i, *_: (0, i, 0)) for o in o_parts] + [
                pl.BlockSpec((w, d), lambda i, *_: (0, 0), pipeline_mode=pl.Buffered(1)),
                pl.BlockSpec((n_p, T, d), lambda i, *_: (0, i, 0)),
            ],
            out_specs=pl.BlockSpec((n_p, T, d), lambda i, *_: (0, i, 0)),
            scratch_shapes=[pltpu.VMEM((n_p * T, w), x.dtype)],
        ),
        compiler_params=pltpu.CompilerParams(dimension_semantics=("arbitrary",), vmem_limit_bytes=VMEM_LIMIT),
        cost_estimate=pl.CostEstimate(flops=2 * n_p * rows * d * w, bytes_accessed=2 * n_p * rows * (d + w), transcendentals=0),
        name="out_local",
    )(valid, *o_parts, w_out, x)


def merge_kernel(valid_ref, first, n_g, *refs):
    y_refs, (cur_ref, out_ref) = refs[:n_g], refs[n_g:]
    kept = valid_ref[first + pl.program_id(0)] == 1

    @pl.when(kept)
    def _():
        out_ref[...] = cur_ref[...]

    @pl.when(jnp.logical_not(kept))
    def _():
        at = 0
        for y_ref in y_refs:
            out_ref[at:at + y_ref.shape[0]] = y_ref[...]
            at += y_ref.shape[0]


def merge(returned, out, valid):
    n_p, rows, d = out.shape
    back = returned[0].shape[1]
    n_g, first = len(returned), (rows - back) // T
    block = pl.BlockSpec((n_p, T, d), lambda i, *_: (0, i + first, 0))
    return pl.pallas_call(
        lambda valid_ref, *refs: merge_kernel(valid_ref, first, n_g, *refs),
        out_shape=jax.ShapeDtypeStruct(out.shape, out.dtype),
        grid_spec=pltpu.PrefetchScalarGridSpec(
            num_scalar_prefetch=1,
            grid=(back // T,),
            in_specs=[pl.BlockSpec((y.shape[0], T, d), lambda i, *_: (0, i, 0)) for y in returned] + [block],
            out_specs=block,
        ),
        input_output_aliases={1 + n_g: 0},
        compiler_params=pltpu.CompilerParams(dimension_semantics=("arbitrary",), vmem_limit_bytes=VMEM_LIMIT),
        name="merge",
    )(valid, *returned, out)


def rotary_tables(positions):
    half = HD // 2
    inv_freq = THETA ** (-jnp.arange(half, dtype=jnp.float32) * 2.0 / HD)
    angles = positions.astype(jnp.float32)[:, None] * inv_freq[None, :]
    cos, sin = jnp.cos(angles), jnp.sin(angles)
    return jnp.concatenate([cos, cos], axis=-1), jnp.concatenate([-sin, sin], axis=-1)


def solution(mesh):
    n_sp = mesh.shape["sp"]

    def block(tokens, w_query, w_key, w_value, w_out, attn_norm, q_norm, k_norm):
        n_p, seq_loc, _ = tokens.shape
        n_kv = w_key.shape[1] // HD
        n_tiles = seq_loc // T
        sizes = []
        while sum(sizes) < n_p:
            sizes.append(min(len(sizes) + 1, n_p - sum(sizes)))
        table = split_work(n_sp, n_tiles)
        spare = max(table)
        me = lax.axis_index("sp")
        gain, q_gain, k_gain = attn_norm.reshape(1, -1), q_norm.reshape(1, -1), k_norm.reshape(1, -1)

        away = [(d, n_sp - 1 - d) for d in range(n_sp) if table[d]]
        x_moved = lax.ppermute(tokens[:, seq_loc - spare * T:, :], "sp", away)

        starts = jnp.concatenate([
            me * seq_loc + jnp.arange(n_tiles) * T,
            (n_sp - me) * seq_loc - spare * T + jnp.arange(spare) * T,
        ])
        cos, sin = rotary_tables((starts[:, None] + jnp.arange(T)[None, :]).reshape(-1))
        info = jnp.asarray(make_info(n_sp, seq_loc, table, DIAG_STEP))[me]

        k, v, pack = kv_project(tokens, w_key, w_value, gain, k_gain, cos, sin)
        kv, at = [], 0
        for s in sizes:
            kv.append(lax.all_gather(pack[at:at + s], "sp"))
            at += s
        total = n_tiles + spare
        q = q_project(tokens, w_query, gain, q_gain, cos, sin, info, 0, total, None)
        q = q_project(x_moved, w_query, gain, q_gain, cos, sin, info, n_tiles, total, q)
        o_parts, returned, at, after = [], [], 0, q
        for s, kv_g in zip(sizes, kv):
            o = attention(q, kv_g, info, after, at, n_kv)
            after = out_moved(o, w_out, x_moved, info, at)
            returned.append(lax.ppermute(after, "sp", [(b, a) for a, b in away]))
            o_parts.append(o)
            at += s
        out = out_local(o_parts, w_out, tokens, info)
        out = merge(returned, out, info)
        return out, k.reshape(n_p, seq_loc, n_kv, HD), v.reshape(n_p, seq_loc, n_kv, HD)

    rows, flat = P("dp", "sp", None), P(None, None)
    cache = P("dp", "sp", None, None)
    return jax.shard_map(
        block,
        mesh=mesh,
        in_specs=(rows, flat, flat, flat, flat, P(None), P(None), P(None)),
        out_specs=(rows, cache, cache),
        check_vma=False,
    )
```

time: 2280 us -> 712 us (0.31)
  the two profiles are of different devices: /device:TPU:112 before, /device:TPU:113 now
where the time goes in v1:
time: 712 us
  Pallas kernels  512 us (72%)
  waiting for transfers between devices  104 us (15%)
  starting transfers between devices  51.2 us (7%)
  local copies, waits for them, and re-layouts  27.6 us (4%)
  between operations  13.9 us (2%)
    pallas_call x3, Pallas kernels, attention(): pl.pallas_call(functools.partial(attn_kernel, n_tiles, grp, bk, DIAG_STEP...  260 us
    pallas_call x2, Pallas kernels, q_project(): pl.pallas_call(functools.partial(q_kernel, first_tile, Q_COLS), out_shape...  109 us
    ppermute x1, waiting for transfers between devices, block(): x_moved = lax.ppermute(tokens[:, seq_loc - spare * T:, :], 'sp', away)  104 us
    pallas_call x1, Pallas kernels, out_local(): pl.pallas_call(functools.partial(out_kernel, n_g, 512), out_shape=jax.Sha...  69 us
    ppermute x3, starting transfers between devices, block(): returned.append(lax.ppermute(after, 'sp', [(b, a) for a, b in away]))  49.5 us
    pallas_call x3, Pallas kernels, out_moved(): pl.pallas_call(functools.partial(out_moved_kernel, 2 * all_rows // T + 1)...  39 us
    pallas_call x1, Pallas kernels, kv_project(): pl.pallas_call(kv_kernel, out_shape=(jax.ShapeDtypeStruct((n_p, rows, w),...  28 us
  transfers between devices with their start and end apart: 7, of which 1 were waited for; matrix products, arithmetic and copies ran while one was open for 3% of the time, Pallas kernels for 67%

profile of v1, /device:TPU:113, one launch (start us, length us, event | category | flops | bytes accessed | tf_op | source)
XLA Modules:
  0.0 711.7 jit_solution(15450217508524747321)
XLA Ops:
  7.3 0.1 pad_add_fusion
  7.4 0.1 add_convert_fusion
  7.4 0.1 convert_element_type.11
  7.5 1.3 reshape.43.g_ref
  8.8 1.3 fusion
  10.1 1.2 pad_maximum_fusion
  11.3 28.0 %kv_proj.1 = (bf16[6,512,512]{2,1,0:T(8,128)(2,1)}, bf16[6,512,512]{2,1,0:T(8,128)(2,1)}, bf16[6,2,512,512]{3,2,1,0:T(8,128)(2,1)}) custom-call(bf16[6,512,2048]{2,1,0:T(8,128)(2,1)} %refs_4_.1, bf16[2048,512]{1,0:T(8,128)(2,1)} %wk_ref.1, bf16[2048,512]{1,0:T(8,128)(2,1)} %wv_ref.1, bf16[1,2048]{1,0:T(2,128)(2,1)} %reshape.43.g_ref, ...), custom_call_target="tpu_custom_call" | custom-call | flops 12884901888 | bytes 50331648 | tf_op jit(solution)/shard_map/kv_proj/pallas_call | solution.py:70
  39.4 2.3 slice.13
  41.7 0.1 all-gather.9.cloned.1.call-start
  41.8 3.0 slice.14
  44.9 0.1 all-gather.11.cloned.1.call-start
  45.0 3.9 slice.15
  48.9 5.9 slice.12
  54.8 1.5 collective-permute-start
  56.3 5.5 reshape.46
  61.8 2.9 reshape.47
  64.8 1.2 constant_dynamic-slice_fusion
  66.0 81.5 %q_proj.2.rest_0_ = bf16[6,704,4096]{2,1,0:T(8,128)(2,1)} custom-call(s32[196]{0:T(256)} %bitcast.6, bf16[6,512,2048]{2,1,0:T(8,128)(2,1)} %refs_4_.1, bf16[2048,4096]{1,0:T(8,128)(2,1)} %w_ref.6, bf16[1,2048]{1,0:T(2,128)(2,1)} %reshape.43.g_ref, bf16[1,128]{1,0:T(2,128)(2,1)} %bitcast.16, f32[704,128]{1,0:T(8,128)} %get-tuple-element.12.cos_ref, ...), custom_call_target="tpu_custom_call" | custom-call | flops 51539607552 | bytes 37748736 | tf_op jit(solution)/shard_map/q_proj/pallas_call | solution.py:140
  147.4 103.8 %collective-permute-done.x_ref = bf16[6,192,2048]{2,1,0:T(8,128)(2,1)} collective-permute-done((bf16[6,192,2048]{2,1,0:T(8,128)(2,1)}, bf16[6,192,2048]{2,1,0:T(8,128)(2,1)}, u32[]{:S(2)}, u32[]{:S(2)}) %collective-permute-start) | collective-permute-done | bytes 4718624 | tf_op jit(solution)/shard_map/ppermute | solution.py:466
  251.2 27.6 %q_proj.3.q_ref.after_ref = bf16[6,704,4096]{2,1,0:T(8,128)(2,1)} custom-call(s32[196]{0:T(256)} %bitcast.7, bf16[6,192,2048]{2,1,0:T(8,128)(2,1)} %collective-permute-done.x_ref, bf16[2048,4096]{1,0:T(8,128)(2,1)} %w_ref.6, bf16[1,2048]{1,0:T(2,128)(2,1)} %reshape.43.g_ref, bf16[1,128]{1,0:T(2,128)(2,1)} %bitcast.17, ...), custom_call_target="tpu_custom_call", output_to_operand_aliasing={{}: (7, {})} | custom-call | flops 19327352832 | bytes 14155776 | tf_op jit(solution)/shard_map/q_proj/pallas_call | solution.py:140
  278.8 47.8 %attn.3.o_ref.refs_0_ = bf16[1,704,4096]{2,1,0:T(8,128)(2,1)} custom-call(s32[196]{0:T(256)} %bitcast.8, bf16[6,704,4096]{2,1,0:T(8,128)(2,1)} %q_proj.3.q_ref.after_ref, bf16[8,1,2,512,512]{4,3,2,1,0:T(8,128)(2,1)} %bitcast.22, bf16[8,1,2,512,512]{4,3,2,1,0:T(8,128)(2,1)} %bitcast.23, bf16[6,704,4096]{2,1,0:T(8,128)(2,1)} %q_proj.3.q_ref.after_ref), custom_call_target="tpu_custom_call" | custom-call | flops 47244640256 | bytes 11534336 | tf_op jit(solution)/shard_map/attn/pallas_call | solution.py:302
  326.7 10.3 %out_moved.3.after_ref = bf16[1,192,2048]{2,1,0:T(8,128)(2,1)} custom-call(s32[196]{0:T(256)} %bitcast.9, bf16[1,704,4096]{2,1,0:T(8,128)(2,1)} %attn.3.o_ref.refs_0_, bf16[4096,2048]{1,0:T(8,128)(2,1)} %refs_3_.1, bf16[6,192,2048]{2,1,0:T(8,128)(2,1)} %collective-permute-done.x_ref), custom_call_target="tpu_custom_call" | custom-call | flops 3221225472 | bytes 16777216 | tf_op jit(solution)/shard_map/out_moved/pallas_call | solution.py:343
  337.0 2.2 collective-permute-start.1
  339.2 86.8 %attn.4.o_ref.refs_1_ = bf16[2,704,4096]{2,1,0:T(8,128)(2,1)} custom-call(s32[196]{0:T(256)} %bitcast.10, bf16[6,704,4096]{2,1,0:T(8,128)(2,1)} %q_proj.3.q_ref.after_ref, bf16[8,2,2,512,512]{4,3,2,1,0:T(8,128)(2,1)} %bitcast.20, bf16[8,2,2,512,512]{4,3,2,1,0:T(8,128)(2,1)} %bitcast.21, bf16[1,192,2048]{2,1,0:T(8,128)(2,1)} %out_moved.3.after_ref), custom_call_target="tpu_custom_call" | custom-call | flops 94489280512 | bytes 23068672 | tf_op jit(solution)/shard_map/attn/pallas_call | solution.py:302
  426.0 12.8 %out_moved.4.after_ref = bf16[2,192,2048]{2,1,0:T(8,128)(2,1)} custom-call(s32[196]{0:T(256)} %bitcast.11, bf16[2,704,4096]{2,1,0:T(8,128)(2,1)} %attn.4.o_ref.refs_1_, bf16[4096,2048]{1,0:T(8,128)(2,1)} %refs_3_.1, bf16[6,192,2048]{2,1,0:T(8,128)(2,1)} %collective-permute-done.x_ref), custom_call_target="tpu_custom_call" | custom-call | flops 6442450944 | bytes 16777216 | tf_op jit(solution)/shard_map/out_moved/pallas_call | solution.py:343
  438.8 16.5 %collective-permute-start.2 = (bf16[2,192,2048]{2,1,0:T(8,128)(2,1)}, bf16[2,192,2048]{2,1,0:T(8,128)(2,1)}, u32[]{:S(2)}, u32[]{:S(2)}) collective-permute-start(bf16[2,192,2048]{2,1,0:T(8,128)(2,1)} %out_moved.4.after_ref), channel_id=1, source_target_pairs={{3,4},{2,5},{1,6},{0,7},{11,12},{10,13},{9,14},{8,15}} | collective-permute-start | bytes 4718600 | tf_op jit(solution)/shard_map/ppermute | solution.py:487
  455.3 125.5 %attn.5.o_ref.refs_2_ = bf16[3,704,4096]{2,1,0:T(8,128)(2,1)} custom-call(s32[196]{0:T(256)} %bitcast.12, bf16[6,704,4096]{2,1,0:T(8,128)(2,1)} %q_proj.3.q_ref.after_ref, bf16[8,3,2,512,512]{4,3,2,1,0:T(8,128)(2,1)} %bitcast.18, bf16[8,3,2,512,512]{4,3,2,1,0:T(8,128)(2,1)} %bitcast.19, bf16[2,192,2048]{2,1,0:T(8,128)(2,1)} %out_moved.4.after_ref), custom_call_target="tpu_custom_call" | custom-call | flops 141733920768 | bytes 34603008 | tf_op jit(solution)/shard_map/attn/pallas_call | solution.py:302
  580.8 16.0 %out_moved.5 = bf16[3,192,2048]{2,1,0:T(8,128)(2,1)} custom-call(s32[196]{0:T(256)} %bitcast.13, bf16[3,704,4096]{2,1,0:T(8,128)(2,1)} %attn.5.o_ref.refs_2_, bf16[4096,2048]{1,0:T(8,128)(2,1)} %refs_3_.1, bf16[6,192,2048]{2,1,0:T(8,128)(2,1)} %collective-permute-done.x_ref), custom_call_target="tpu_custom_call" | custom-call | flops 9663676416 | bytes 16777216 | tf_op jit(solution)/shard_map/out_moved/pallas_call | solution.py:343
  596.7 30.8 %collective-permute-start.3 = (bf16[3,192,2048]{2,1,0:T(8,128)(2,1)}, bf16[3,192,2048]{2,1,0:T(8,128)(2,1)S(1)}, u32[]{:S(2)}, u32[]{:S(2)}) collective-permute-start(bf16[3,192,2048]{2,1,0:T(8,128)(2,1)} %out_moved.5), channel_id=1, source_target_pairs={{3,4},{2,5},{1,6},{0,7},{11,12},{10,13},{9,14},{8,15}} | collective-permute-start | bytes 7077896 | tf_op jit(solution)/shard_map/ppermute | solution.py:487
  627.6 69.0 %out_local.1.refs_3_ = bf16[6,512,2048]{2,1,0:T(8,128)(2,1)} custom-call(s32[196]{0:T(256)} %bitcast.14, bf16[1,704,4096]{2,1,0:T(8,128)(2,1)} %attn.3.o_ref.refs_0_, bf16[2,704,4096]{2,1,0:T(8,128)(2,1)} %attn.4.o_ref.refs_1_, bf16[3,704,4096]{2,1,0:T(8,128)(2,1)} %attn.5.o_ref.refs_2_, bf16[4096,2048]{1,0:T(8,128)(2,1)} %refs_3_.1, ...), custom_call_target="tpu_custom_call" | custom-call | flops 51539607552 | bytes 37748736 | tf_op jit(solution)/shard_map/out_local/pallas_call | solution.py:387
  696.6 1.4 copy-done.1
  698.0 7.2 %merge.1 = bf16[6,512,2048]{2,1,0:T(8,128)(2,1)} custom-call(s32[196]{0:T(256)} %bitcast.15, bf16[1,192,2048]{2,1,0:T(8,128)(2,1)} %collective-permute-done.1.refs_0_, bf16[2,192,2048]{2,1,0:T(8,128)(2,1)} %collective-permute-done.2.refs_1_, bf16[3,192,2048]{2,1,0:T(8,128)(2,1)} %copy-done.1, ...), custom_call_target="tpu_custom_call", output_to_operand_aliasing={{}: (4, {})} | custom-call | tf_op jit(solution)/shard_map/merge/pallas_call | solution.py:427
  (16 shorter events, 0.3 us)
Async XLA Ops:
  7.2 271.7 %all-gather.7.cloned.1.call-start = ((), (), s32[]{:S(2)}) async-start(), calls=%async_computation | async-start | bytes 9437184 | tf_op jit(solution)/shard_map/all_gather | solution.py:478
  41.7 297.5 %all-gather.9.cloned.1.call-start = ((), (), s32[]{:S(2)}) async-start(), calls=%async_computation.1 | async-start | bytes 18874368 | tf_op jit(solution)/shard_map/all_gather | solution.py:478
  44.9 410.4 %all-gather.11.cloned.1.call-start = ((), (), s32[]{:S(2)}) async-start(), calls=%async_computation.2 | async-start | bytes 28311552 | tf_op jit(solution)/shard_map/all_gather | solution.py:478
  48.9 12.9 %copy-start = (bf16[6,512,512]{2,1,0:T(8,128)(2,1)S(1)}, bf16[6,512,512]{2,1,0:T(8,128)(2,1)}, u32[]{:S(2)}) copy-start(bf16[6,512,512]{2,1,0:T(8,128)(2,1)} %get-tuple-element.8) | copy-start | bytes 9437188
  54.8 196.4 %collective-permute-start = (bf16[6,192,2048]{2,1,0:T(8,128)(2,1)}, bf16[6,192,2048]{2,1,0:T(8,128)(2,1)}, u32[]{:S(2)}, u32[]{:S(2)}) collective-permute-start(bf16[6,192,2048]{2,1,0:T(8,128)(2,1)} %slice.12), channel_id=1, source_target_pairs={{4,3},{5,2},{6,1},{7,0},{12,11},{13,10},{14,9},{15,8}} | collective-permute-start | bytes 14155784 | tf_op jit(solution)/shard_map/ppermute | solution.py:466
  337.0 359.5 %collective-permute-start.1 = (bf16[1,192,2048]{2,1,0:T(8,128)(2,1)}, bf16[1,192,2048]{2,1,0:T(8,128)(2,1)}, u32[]{:S(2)}, u32[]{:S(2)}) collective-permute-start(bf16[1,192,2048]{2,1,0:T(8,128)(2,1)} %out_moved.3.after_ref), channel_id=1, source_target_pairs={{3,4},{2,5},{1,6},{0,7},{11,12},{10,13},{9,14},{8,15}} | collective-permute-start | bytes 2359304 | tf_op jit(solution)/shard_map/ppermute | solution.py:487
  438.8 257.7 %collective-permute-start.2 = (bf16[2,192,2048]{2,1,0:T(8,128)(2,1)}, bf16[2,192,2048]{2,1,0:T(8,128)(2,1)}, u32[]{:S(2)}, u32[]{:S(2)}) collective-permute-start(bf16[2,192,2048]{2,1,0:T(8,128)(2,1)} %out_moved.4.after_ref), channel_id=1, source_target_pairs={{3,4},{2,5},{1,6},{0,7},{11,12},{10,13},{9,14},{8,15}} | collective-permute-start | bytes 4718600 | tf_op jit(solution)/shard_map/ppermute | solution.py:487
  596.7 99.8 %collective-permute-start.3 = (bf16[3,192,2048]{2,1,0:T(8,128)(2,1)}, bf16[3,192,2048]{2,1,0:T(8,128)(2,1)S(1)}, u32[]{:S(2)}, u32[]{:S(2)}) collective-permute-start(bf16[3,192,2048]{2,1,0:T(8,128)(2,1)} %out_moved.5), channel_id=1, source_target_pairs={{3,4},{2,5},{1,6},{0,7},{11,12},{10,13},{9,14},{8,15}} | collective-permute-start | bytes 7077896 | tf_op jit(solution)/shard_map/ppermute | solution.py:487
  696.5 1.4 copy-start.1
Sparse Core Ops, SparseCore 0:
  41.8 76.2 all-gather.6
  119.8 139.8 all-gather.8
  261.3 127.4 all-gather.10

commit v2 on v1

v2 whole, which is shorter than its diff:
```python
import functools
import math

import jax
import jax.numpy as jnp
import numpy as np
from jax import lax
from jax.experimental import pallas as pl
from jax.experimental.pallas import tpu as pltpu
from jax.sharding import PartitionSpec as P

EPS = 1e-6
THETA = 1000000.0
HD = 128
T = 64
VMEM_LIMIT = 60 * 1024 * 1024
Q_COLS = 512
DIAG_STEP = 256
TILE_COST, TAKEN_COST, ITEM_COST = 17.0, 25.0, 7.5


def split_work(n_sp, n_tiles):
    moved = [0] * n_sp
    for d in range((n_sp + 1) // 2, n_sp):
        low = n_sp - 1 - d
        high, small = ITEM_COST * (d + 1), ITEM_COST * (low + 1)
        moved[d] = min(
            range(n_tiles // 2 + 1),
            key=lambda k: max((n_tiles - k) * (TILE_COST + high), n_tiles * (TILE_COST + small) + k * (TAKEN_COST + high)),
        )
    return moved


def normed(x_ref, gain_ref):
    p, r, d = x_ref.shape
    x = x_ref[...].reshape(p * r, d).astype(jnp.float32)
    inv = lax.rsqrt(jnp.mean(x * x, axis=-1, keepdims=True) + EPS)
    return (x * inv * gain_ref[...].astype(jnp.float32)).astype(jnp.bfloat16)


def head_norm_rope(y, gain, cos, sin, n_rep):
    inv = lax.rsqrt(jnp.mean(y * y, axis=-1, keepdims=True) + EPS)
    y = y * inv * gain
    rolled = pltpu.roll(y, HD // 2, 1)
    r = cos.shape[0]
    y, rolled = y.reshape(n_rep, r, HD), rolled.reshape(n_rep, r, HD)
    return (y * cos[None] + rolled * sin[None]).astype(jnp.bfloat16)


def kv_kernel(sizes, x_ref, wk_ref, wv_ref, g_ref, kg_ref, cos_ref, sin_ref, k_ref, v_ref, h_ref, *pack_refs):
    n_p, r, d = x_ref.shape
    i = pl.program_id(0)
    h = normed(x_ref, g_ref)
    h_ref[...] = h.reshape(n_p, r, d)
    k = jnp.dot(h, wk_ref[...], preferred_element_type=jnp.float32).astype(jnp.bfloat16).astype(jnp.float32)
    v = jnp.dot(h, wv_ref[...], preferred_element_type=jnp.float32).astype(jnp.bfloat16)
    gain = kg_ref[...].astype(jnp.float32)
    cos, sin = cos_ref[...], sin_ref[...]
    rows = pl.ds(pl.multiple_of(i * r, r), r)
    v_ref[...] = v.reshape(v_ref.shape)
    at = 0
    for size, pack_ref in zip(sizes, pack_refs):
        for p in range(size):
            pack_ref[p, 1, :, rows] = v[(at + p) * r:(at + p + 1) * r].T
        at += size
    for j in range(k.shape[1] // HD):
        cols = slice(j * HD, (j + 1) * HD)
        y = head_norm_rope(k[:, cols], gain, cos, sin, n_p)
        k_ref[:, :, cols] = y
        at = 0
        for size, pack_ref in zip(sizes, pack_refs):
            pack_ref[:, 0, rows, cols] = y[at:at + size]
            at += size


def kv_project(x, w_key, w_value, gain, k_gain, cos, sin, sizes):
    n_p, rows, d = x.shape
    w = w_key.shape[1]
    r = min(128, rows)
    whole = lambda shape: pl.BlockSpec(shape, lambda i: (0,) * len(shape))
    cut = lambda cols: pl.BlockSpec((n_p, r, cols), lambda i: (0, i, 0))
    packs = [(s, 2, rows, w) for s in sizes]
    return pl.pallas_call(
        functools.partial(kv_kernel, sizes),
        out_shape=[jax.ShapeDtypeStruct(s, x.dtype) for s in [(n_p, rows, w)] * 2 + [(n_p, rows, d)] + packs],
        grid=(rows // r,),
        in_specs=[
            cut(d), whole((d, w)), whole((d, w)), whole((1, d)), whole((1, HD)),
            pl.BlockSpec((r, HD), lambda i: (i, 0)), pl.BlockSpec((r, HD), lambda i: (i, 0)),
        ],
        out_specs=[cut(w), cut(w), cut(d)] + [whole(s) for s in packs],
        compiler_params=pltpu.CompilerParams(dimension_semantics=("arbitrary",), vmem_limit_bytes=VMEM_LIMIT),
        cost_estimate=pl.CostEstimate(flops=4 * n_p * rows * d * w, bytes_accessed=8 * n_p * rows * d, transcendentals=0),
        name="kv_proj",
    )(x, w_key, w_value, gain, k_gain, cos, sin)


def q_kernel(nc, is_normed, step_of, info_ref, x_ref, w_ref, g_ref, qg_ref, cos_ref, sin_ref, after_ref, q_ref, h_scr, y_scr, w_scr, sem):
    n_p, r, d = x_ref.shape
    i = pl.program_id(0)
    begin, first_tile = step_of(info_ref)
    n_chunks = w_ref.shape[1] // nc

    def cols(n):
        return pl.ds(pl.multiple_of(n * nc, nc), nc)

    def load(n):
        return pltpu.make_async_copy(w_ref.at[:, cols(n)], w_scr.at[:, cols(n)], sem.at[n])

    @pl.when((info_ref[first_tile + i] == 1) & (i >= begin))
    def _():
        @pl.when(i == begin)
        def _():
            for n in range(n_chunks):
                load(n).start()

        h_scr[...] = x_ref[...].reshape(n_p * r, d) if is_normed else normed(x_ref, g_ref)
        gain = qg_ref[...].astype(jnp.float32) * (math.log2(math.e) / math.sqrt(HD))
        cos, sin = cos_ref[...], sin_ref[...]

        def arrived(n):
            @pl.when(i == begin)
            def _():
                load(n).wait()

        def project(n):
            y_scr[...] = jnp.dot(h_scr[...], w_scr[:, cols(n)], preferred_element_type=jnp.float32).astype(jnp.bfloat16)

        def finish(n):
            for j in range(nc // HD):
                y = head_norm_rope(y_scr[:, j * HD:(j + 1) * HD].astype(jnp.float32), gain, cos, sin, n_p)
                q_ref[:, :, pl.ds(pl.multiple_of(n * nc + j * HD, HD), HD)] = y

        def step(n, _):
            arrived(n + 1)
            finish(n)
            project(n + 1)
            return 0

        arrived(0)
        project(0)
        lax.fori_loop(0, n_chunks - 1, step, 0)
        finish(n_chunks - 1)


def q_project(x, w_query, gain, q_gain, cos, sin, info, first_tile, total_tiles, is_normed, after):
    n_p, rows, d = x.shape
    w = w_query.shape[1]
    n_tiles = rows // T
    begin = lambda info: n_tiles - info[2 * total_tiles + 2] if first_tile else 0
    local = lambda i, info: jnp.minimum(jnp.maximum(i, begin(info)), n_tiles - 1)
    whole = lambda shape: pl.BlockSpec(shape, lambda i, info: (0,) * len(shape))
    table = pl.BlockSpec((T, HD), lambda i, info: (local(i, info) + first_tile, 0))
    nc = Q_COLS
    return pl.pallas_call(
        functools.partial(q_kernel, nc, is_normed, lambda info: (begin(info), first_tile)),
        out_shape=jax.ShapeDtypeStruct((n_p, rows, w), x.dtype),
        grid_spec=pltpu.PrefetchScalarGridSpec(
            num_scalar_prefetch=1,
            grid=(n_tiles,),
            in_specs=[
                pl.BlockSpec((n_p, T, d), lambda i, info: (0, local(i, info), 0)),
                pl.BlockSpec(memory_space=pl.ANY),
                whole((1, d)), whole((1, HD)), table, table,
                pl.BlockSpec(memory_space=pl.ANY),
            ],
            out_specs=pl.BlockSpec((n_p, T, w), lambda i, info: (0, local(i, info), 0)),
            scratch_shapes=[
                pltpu.VMEM((n_p * T, d), x.dtype), pltpu.VMEM((n_p * T, nc), x.dtype),
                pltpu.VMEM((d, w), x.dtype), pltpu.SemaphoreType.DMA((w // nc,)),
            ],
        ),
        compiler_params=pltpu.CompilerParams(dimension_semantics=("arbitrary",), vmem_limit_bytes=VMEM_LIMIT),
        cost_estimate=pl.CostEstimate(flops=2 * n_p * rows * d * w, bytes_accessed=2 * n_p * rows * (d + w), transcendentals=0),
        name="q_proj",
    )(info, x, w_query, gain, q_gain, cos, sin, after)


def attn_kernel(n_tiles, parts, grp, bk, ext_step, hp, ck, info_ref, *refs):
    n_q = len(parts)
    q_refs, (k_ref, v_ref, _), o_refs = refs[:n_q], refs[n_q:n_q + 3], refs[n_q + 3:2 * n_q + 3]
    q_scr, s_scr, bm_scr, m_scr, l_scr, acc_scr = refs[2 * n_q + 3:]
    first_tile = parts[0][0]
    n = grp * T
    base = 2 * n_tiles + 3
    m_items = (info_ref.shape[0] - base) // 4

    def tile(i): return info_ref[base + i]

    def blk(i): return info_ref[base + m_items + i]

    def first(i): return info_ref[base + 2 * m_items + i]

    def diag(i): return info_ref[base + 3 * m_items + i]

    @pl.when((pl.program_id(0) == 0) & (pl.program_id(1) == 0))
    def _():
        l_scr[...] = jnp.zeros_like(l_scr)
        acc_scr[...] = jnp.zeros_like(acc_scr)
        m_scr[...] = jnp.zeros_like(m_scr)

    for h in range(hp):
        for (start, tiles), q_ref in zip(parts, q_refs):
            for t in range(tiles):
                for j in range(grp):
                    q_scr[h, start - first_tile + t, j * T:(j + 1) * T, :] = q_ref[0, t * T:(t + 1) * T, (h * grp + j) * HD:(h * grp + j + 1) * HD]

    def fold(x, op):
        return op(x.reshape(x.shape[0] // 8, 8, n), axis=0)

    def qk_chunk(i, h, r):
        s = lax.dot_general(k_ref[blk(i), r * ck:(r + 1) * ck, h * HD:(h + 1) * HD], q_scr[h, jnp.clip(tile(i) - first_tile, 0, q_scr.shape[1] - 1)], (((1,), (1,)), ((), ())), preferred_element_type=jnp.float32)
        s_scr[h, r * ck:(r + 1) * ck, :] = s
        return fold(s, jnp.max)

    def masked_chunk(i, h, r, ext):
        s = s_scr[h, r * ck:r * ck + ext, :]
        off = info_ref[n_tiles + tile(i)] - blk(i) * bk - r * ck
        row = lax.broadcasted_iota(jnp.int32, (ext, n), 0)
        col = lax.broadcasted_iota(jnp.int32, (ext, n), 1) & (T - 1)
        return jnp.where(row - col <= off, s, -jnp.inf)

    def body(i, ext, masked):
        b = blk(i)
        fresh = first(i) == 1
        for h in range(hp):
            if masked:
                bm = jnp.full((8, n), -jnp.inf, jnp.float32)
                for r in range(bk // ck):
                    e = min(ck, ext - r * ck)
                    if e <= 0:
                        continue
                    if r * ck + e > ext - ext_step:
                        sm = masked_chunk(i, h, r, e)
                        s_scr[h, r * ck:r * ck + e, :] = sm
                    else:
                        sm = s_scr[h, r * ck:r * ck + e, :]
                    bm = jnp.maximum(bm, fold(sm, jnp.max))
            else:
                bm = bm_scr[h]
            m_old = jnp.where(fresh, -jnp.inf, m_scr[h])
            m_new = jnp.maximum(m_old, jnp.max(bm, axis=0, keepdims=True))
            m_scr[h] = m_new
            alpha = jnp.exp2(m_old - m_new)
            l = l_scr[h] * alpha
            pv = None
            bm_next = None
            for r in range(bk // ck):
                e = min(ck, ext - r * ck)
                if e > 0:
                    p = jnp.exp2(s_scr[h, r * ck:r * ck + e, :] - m_new)
                    l = l + fold(p, jnp.sum)
                    d = jnp.dot(v_ref[b, h * HD:(h + 1) * HD, r * ck:r * ck + e], p.astype(jnp.bfloat16), preferred_element_type=jnp.float32)
                    pv = d if pv is None else pv + d
                x = qk_chunk(i + 1, h, r)
                bm_next = x if bm_next is None else jnp.maximum(bm_next, x)
            l_scr[h] = l
            bm_scr[h] = bm_next
            acc_scr[h] = acc_scr[h] * alpha + pv

    def finish(i):
        t = tile(i)
        for h in range(hp):
            inv = 1.0 / jnp.sum(l_scr[h], axis=0, keepdims=True)
            o = (acc_scr[h] * inv).T.astype(jnp.bfloat16)
            for (start, tiles), o_ref in zip(parts, o_refs):
                @pl.when((t >= start) & (t < start + tiles))
                def _():
                    at = pl.ds(pl.multiple_of((t - start) * T, T), T)
                    for j in range(grp):
                        o_ref[0, at, (h * grp + j) * HD:(h * grp + j + 1) * HD] = o[j * T:(j + 1) * T]

    begin = 0 if first_tile == 0 else info_ref[2 * n_tiles]
    end = info_ref[2 * n_tiles + (1 if n_q > 1 or first_tile else 0)]

    @pl.when(end > begin)
    def _():
        for h in range(hp):
            bm = None
            for r in range(bk // ck):
                x = qk_chunk(begin, h, r)
                bm = x if bm is None else jnp.maximum(bm, x)
            bm_scr[h] = bm

        def step(i, _):
            d = diag(i)

            @pl.when(d == 0)
            def _():
                body(i, bk, False)

            for e in range(bk // ext_step):
                @pl.when(d == e + 1)
                def _():
                    body(i, (e + 1) * ext_step, True)
                    finish(i)
            return 0

        lax.fori_loop(begin, end, step, 0)


def make_info(n_sp, seq_loc, moved, ext_step):
    n_tiles, spare = seq_loc // T, max(moved)
    rows = []
    for me in range(n_sp):
        other = n_sp - 1 - me
        pos = [me * seq_loc + t * T for t in range(n_tiles)]
        pos += [(other + 1) * seq_loc - (spare - t) * T for t in range(spare)]
        valid = [t < n_tiles - moved[me] for t in range(n_tiles)] + [t >= spare - moved[other] for t in range(spare)]
        items = []
        for t, p in enumerate(pos):
            if valid[t]:
                last = p // seq_loc
                for b in range(last + 1):
                    items.append((t, b, int(b == 0), (p - last * seq_loc) // ext_step + 1 if b == last else 0))
        own = sum(t < n_tiles for t, *_ in items)
        rows.append(([int(v) for v in valid] + pos + [own, len(items), moved[other]], items))
    m = max(len(items) for _, items in rows) + 1
    out = []
    for head, items in rows:
        items = items + [(0, 0, 0, 0)] * (m - len(items))
        out.append(head + [item[k] for k in range(4) for item in items])
    return np.asarray(out, np.int32)


def attention(qs, firsts, kv, info, after, first_prompt, n_kv, total_tiles, hp=4, ck=256):
    width = qs[0].shape[2]
    grp = width // HD // n_kv
    n_dev, nb, _, bk, _ = kv.shape
    parts = [(f, q.shape[1] // T) for f, q in zip(firsts, qs)]
    n_tiles = sum(t for _, t in parts)
    n = grp * T
    flops = 2 * 4 * nb * n_tiles * T * width * n_dev * bk // 2
    return pl.pallas_call(
        functools.partial(attn_kernel, total_tiles, parts, grp, bk, DIAG_STEP, hp, ck),
        out_shape=[jax.ShapeDtypeStruct((nb,) + q.shape[1:], q.dtype) for q in qs],
        grid_spec=pltpu.PrefetchScalarGridSpec(
            num_scalar_prefetch=1,
            grid=(nb, n_kv // hp),
            in_specs=[pl.BlockSpec((1, q.shape[1], hp * grp * HD), lambda p, h, *_: (p + first_prompt, 0, h)) for q in qs] + [
                pl.BlockSpec((n_dev, None, None, bk, hp * HD), lambda p, h, *_: (0, p, 0, 0, h)),
                pl.BlockSpec((n_dev, None, None, hp * HD, bk), lambda p, h, *_: (0, p, 1, h, 0)),
                pl.BlockSpec(memory_space=pl.ANY),
            ],
            out_specs=[pl.BlockSpec((1, q.shape[1], hp * grp * HD), lambda p, h, *_: (p, 0, h)) for q in qs],
            scratch_shapes=[
                pltpu.VMEM((hp, n_tiles, n, HD), qs[0].dtype),
                pltpu.VMEM((hp, bk, n), jnp.float32),
                pltpu.VMEM((hp, 8, n), jnp.float32),
                pltpu.VMEM((hp, 1, n), jnp.float32),
                pltpu.VMEM((hp, 8, n), jnp.float32),
                pltpu.VMEM((hp, HD, n), jnp.float32),
            ],
        ),
        compiler_params=pltpu.CompilerParams(dimension_semantics=("arbitrary", "arbitrary"), vmem_limit_bytes=VMEM_LIMIT),
        cost_estimate=pl.CostEstimate(flops=flops, bytes_accessed=4 * nb * n_tiles * T * width, transcendentals=0),
        name="attn",
    )(info, *qs, kv, kv, after)


def out_moved_kernel(taken, n_o, info_ref, *refs):
    o_refs, (w_ref, x_ref, y_ref) = refs[:n_o], refs[n_o:]

    @pl.when(info_ref[taken] > 0)
    def _():
        n_p, r, _ = x_ref.shape
        o = [o_ref[...].reshape(-1, o_ref.shape[2]) for o_ref in o_refs]
        y = jnp.dot(jnp.concatenate(o, axis=0), w_ref[...], preferred_element_type=jnp.float32)
        y_ref[...] = (x_ref[...].astype(jnp.float32) + y.reshape(n_p, r, -1)).astype(y_ref.dtype)


def out_moved(o_parts, w_out, x, info, first_prompt, total_tiles):
    _, rows, w = o_parts[0].shape
    nb = sum(o.shape[0] for o in o_parts)
    d = x.shape[2]
    nc = min(512, d)
    taken = 2 * total_tiles + 2
    col = lambda i, info: i * jnp.minimum(info[taken], 1)
    return pl.pallas_call(
        functools.partial(out_moved_kernel, taken, len(o_parts)),
        out_shape=jax.ShapeDtypeStruct((nb, rows, d), x.dtype),
        grid_spec=pltpu.PrefetchScalarGridSpec(
            num_scalar_prefetch=1,
            grid=(d // nc,),
            in_specs=[pl.BlockSpec(o.shape, lambda i, *_: (0, 0, 0)) for o in o_parts] + [
                pl.BlockSpec((w, nc), lambda i, info: (0, col(i, info))),
                pl.BlockSpec((pl.Element(nb), pl.Element(rows), pl.Element(nc)), lambda i, info: (first_prompt, 0, col(i, info) * nc)),
            ],
            out_specs=pl.BlockSpec((nb, rows, nc), lambda i, info: (0, 0, col(i, info))),
        ),
        compiler_params=pltpu.CompilerParams(dimension_semantics=("arbitrary",), vmem_limit_bytes=VMEM_LIMIT),
        cost_estimate=pl.CostEstimate(flops=2 * nb * rows * d * w, bytes_accessed=2 * w * d, transcendentals=0),
        name="out_moved",
    )(info, *o_parts, w_out, x)


def out_kernel(n_g, nc, info_ref, *refs):
    o_refs, (w_ref, x_ref, _, y_ref, o_scr, w_scr, sem) = refs[:n_g], refs[n_g:]
    i = pl.program_id(0)
    n_chunks = w_ref.shape[1] // nc

    def load(n):
        cols = slice(n * nc, (n + 1) * nc)
        return pltpu.make_async_copy(w_ref.at[:, cols], w_scr.at[:, cols], sem.at[n])

    @pl.when(i == 0)
    def _():
        for n in range(n_chunks):
            load(n).start()

    @pl.when(info_ref[i] == 1)
    def _():
        n_p, r, _ = x_ref.shape
        at = 0
        for o_ref in o_refs:
            nb, _, w = o_ref.shape
            o_scr[at:at + nb * r, :] = o_ref[...].reshape(nb * r, w)
            at += nb * r

        for n in range(n_chunks):
            @pl.when(i == 0)
            def _():
                load(n).wait()

            cols = slice(n * nc, (n + 1) * nc)
            y = jnp.dot(o_scr[...], w_scr[:, cols], preferred_element_type=jnp.float32)
            y_ref[:, :, cols] = (x_ref[:, :, cols].astype(jnp.float32) + y.reshape(n_p, r, nc)).astype(y_ref.dtype)


def out_local(o_parts, w_out, x, info, after):
    n_p, rows, d = x.shape
    w = o_parts[0].shape[2]
    n_g, nc = len(o_parts), min(1024, d)
    return pl.pallas_call(
        functools.partial(out_kernel, n_g, nc),
        out_shape=jax.ShapeDtypeStruct(x.shape, x.dtype),
        grid_spec=pltpu.PrefetchScalarGridSpec(
            num_scalar_prefetch=1,
            grid=(rows // T,),
            in_specs=[pl.BlockSpec((o.shape[0], T, w), lambda i, *_: (0, i, 0)) for o in o_parts] + [
                pl.BlockSpec(memory_space=pl.ANY),
                pl.BlockSpec((n_p, T, d), lambda i, *_: (0, i, 0)),
                pl.BlockSpec(memory_space=pl.ANY),
            ],
            out_specs=pl.BlockSpec((n_p, T, d), lambda i, *_: (0, i, 0)),
            scratch_shapes=[pltpu.VMEM((n_p * T, w), x.dtype), pltpu.VMEM((w, d), x.dtype), pltpu.SemaphoreType.DMA((d // nc,))],
        ),
        compiler_params=pltpu.CompilerParams(dimension_semantics=("arbitrary",), vmem_limit_bytes=VMEM_LIMIT),
        cost_estimate=pl.CostEstimate(flops=2 * n_p * rows * d * w, bytes_accessed=2 * n_p * rows * (d + w), transcendentals=0),
        name="out_local",
    )(info, *o_parts, w_out, x, after)


def merge_kernel(n_g, given_ref, *refs):
    y_refs, (cur_ref, out_ref) = refs[:n_g], refs[n_g:]

    @pl.when(given_ref[0] == 0)
    def _():
        out_ref[...] = cur_ref[...]

    @pl.when(given_ref[0] > 0)
    def _():
        at = 0
        for y_ref in y_refs:
            out_ref[at:at + y_ref.shape[0]] = y_ref[...]
            at += y_ref.shape[0]


def merge(returned, out, given):
    n_p, rows, d = out.shape
    back, n_tiles = returned[0].shape[1] // T, rows // T
    n_g = len(returned)
    at = lambda i, given: jnp.minimum(jnp.maximum(i, back - given[0]), back - 1)
    block = pl.BlockSpec((n_p, T, d), lambda i, given: (0, n_tiles - back + at(i, given), 0))
    return pl.pallas_call(
        functools.partial(merge_kernel, n_g),
        out_shape=jax.ShapeDtypeStruct(out.shape, out.dtype),
        grid_spec=pltpu.PrefetchScalarGridSpec(
            num_scalar_prefetch=1,
            grid=(back,),
            in_specs=[pl.BlockSpec((y.shape[0], T, d), lambda i, given: (0, at(i, given), 0)) for y in returned] + [block],
            out_specs=block,
        ),
        input_output_aliases={1 + n_g: 0},
        compiler_params=pltpu.CompilerParams(dimension_semantics=("arbitrary",), vmem_limit_bytes=VMEM_LIMIT),
        name="merge",
    )(given, *returned, out)


def rotary_tables(positions):
    half = HD // 2
    inv_freq = THETA ** (-jnp.arange(half, dtype=jnp.float32) * 2.0 / HD)
    angles = positions.astype(jnp.float32)[:, None] * inv_freq[None, :]
    cos, sin = jnp.cos(angles), jnp.sin(angles)
    return jnp.concatenate([cos, cos], axis=-1), jnp.concatenate([-sin, sin], axis=-1)


def solution(mesh):
    n_sp = mesh.shape["sp"]

    def block(tokens, w_query, w_key, w_value, w_out, attn_norm, q_norm, k_norm):
        n_p, seq_loc, _ = tokens.shape
        n_kv = w_key.shape[1] // HD
        n_tiles = seq_loc // T
        sizes = []
        while sum(sizes) < n_p:
            sizes.append(min(len(sizes) + 1, n_p - sum(sizes)))
        table = split_work(n_sp, n_tiles)
        spare = max(table)
        me = lax.axis_index("sp")
        gain, q_gain, k_gain = attn_norm.reshape(1, -1), q_norm.reshape(1, -1), k_norm.reshape(1, -1)

        away = [(d, n_sp - 1 - d) for d in range(n_sp) if table[d]]
        x_moved = lax.ppermute(tokens[:, seq_loc - spare * T:, :], "sp", away)

        starts = jnp.concatenate([
            me * seq_loc + jnp.arange(n_tiles) * T,
            (n_sp - me) * seq_loc - spare * T + jnp.arange(spare) * T,
        ])
        cos, sin = rotary_tables((starts[:, None] + jnp.arange(T)[None, :]).reshape(-1))
        info = jnp.asarray(make_info(n_sp, seq_loc, table, DIAG_STEP))[me]

        given = jnp.asarray(table, jnp.int32)[me].reshape(1)
        k, v, h, *packs = kv_project(tokens, w_key, w_value, gain, k_gain, cos, sin, sizes)
        kv = [lax.all_gather(pack, "sp") for pack in packs]
        total = n_tiles + spare
        q = q_project(h, w_query, gain, q_gain, cos, sin, info, 0, total, True, info)
        k, v, q = lax.optimization_barrier((k, v, q))
        own, extra, at = [], [], sizes[0]
        (o,) = attention([q], [0], kv[0], info, info, 0, n_kv, total)
        own.append(o)
        q_x = q_project(x_moved, w_query, gain, q_gain, cos, sin, info, n_tiles, total, False, o)
        (o_x,) = attention([q_x], [n_tiles], kv[0], info, info, 0, n_kv, total)
        extra.append(o_x)
        after, done, returned = o_x, 0, []
        for g in range(1, len(sizes)):
            o, o_x = attention([q, q_x], [0, n_tiles], kv[g], info, after, at, n_kv, total)
            at += sizes[g]
            own.append(o)
            extra.append(o_x)
            after = out_moved(extra, w_out, x_moved, info, done, total)
            returned.append(lax.ppermute(after, "sp", [(b, a) for a, b in away]))
            done, extra = at, []
        out = out_local(own, w_out, tokens, info, after)
        out = merge(returned, out, given)
        return out, k.reshape(n_p, seq_loc, n_kv, HD), v.reshape(n_p, seq_loc, n_kv, HD)

    rows, flat = P("dp", "sp", None), P(None, None)
    cache = P("dp", "sp", None, None)
    return jax.shard_map(
        block,
        mesh=mesh,
        in_specs=(rows, flat, flat, flat, flat, P(None), P(None), P(None)),
        out_specs=(rows, cache, cache),
        check_vma=False,
    )
```

time: 712 us -> 682 us (0.958)
  the two profiles are of different devices: /device:TPU:113 before, /device:TPU:112 now
where the time goes in v2:
time: 682 us; the launch traced here: 674 us
  Pallas kernels  546 us (80%)
  waiting for transfers between devices  85.6 us (13%)
  local copies, waits for them, and re-layouts  19.3 us (3%)
  between operations  14.4 us (2%)
    pallas_call x4, Pallas kernels, attention(): pl.pallas_call(functools.partial(attn_kernel, total_tiles, parts, grp, bk...  307 us
    pallas_call x2, Pallas kernels, q_project(): pl.pallas_call(functools.partial(q_kernel, nc, is_normed, lambda info: (b...  109 us
    ppermute x1, waiting for transfers between devices, block(): x_moved = lax.ppermute(tokens[:, seq_loc - spare * T:, :], 'sp', away)  84 us
    pallas_call x1, Pallas kernels, out_local(): pl.pallas_call(functools.partial(out_kernel, n_g, nc), out_shape=jax.Shap...  64.5 us
    pallas_call x2, Pallas kernels, out_moved(): pl.pallas_call(functools.partial(out_moved_kernel, taken, len(o_parts)),...  31.8 us
    pallas_call x1, Pallas kernels, kv_project(): pl.pallas_call(functools.partial(kv_kernel, sizes), out_shape=[jax.ShapeD...  29.3 us
  transfers between devices with their start and end apart: 6, of which 1 were waited for; matrix products, arithmetic and copies ran while one was open for 2% of the time, Pallas kernels for 76%

profile of v2, /device:TPU:112, one launch (start us, length us, event | category | flops | bytes accessed | tf_op | source)
XLA Modules:
  0.0 673.8 jit_solution(15093936242015228417)
XLA Ops:
  7.2 0.1 all-gather.7.cloned.1.call-start
  7.3 0.1 pad_add_fusion
  7.4 0.1 add_convert_fusion
  7.4 0.1 convert_element_type.11
  7.5 1.3 reshape.43.g_ref
  8.8 1.3 fusion
  10.1 1.1 pad_maximum_fusion
  11.3 29.3 %kv_proj.1 = (bf16[6,512,512]{2,1,0:T(8,128)(2,1)}, bf16[6,512,512]{2,1,0:T(8,128)(2,1)}, bf16[6,512,2048]{2,1,0:T(8,128)(2,1)}, bf16[1,2,512,512]{3,2,1,0:T(8,1...) custom-call(bf16[6,512,2048]{2,1,0:T(8,128)(2,1)} %refs_4_.1, bf16[2048,512]{1,0:T(8,128)(2,1)} %wk_ref.1, ...), custom_call_target="tpu_custom_call" | custom-call | flops 12884901888 | bytes 50331648 | tf_op jit(solution)/shard_map/kv_proj/pallas_call | solution.py:83
  40.6 0.1 all-gather.9.cloned.1.call-start
  40.7 0.7 all-gather.9.cloned.1.call-update
  41.4 0.1 all-gather.11.cloned.1.call-start
  41.5 0.7 all-gather.11.cloned.1.call-update
  42.2 5.2 slice.3
  47.4 1.3 collective-permute-start
  48.7 1.3 constant_dynamic-slice_fusion
  50.0 75.7 %q_proj.2.refs_0_ = bf16[6,512,4096]{2,1,0:T(8,128)(2,1)} custom-call(s32[197]{0:T(256)} %bitcast.6, bf16[6,512,2048]{2,1,0:T(8,128)(2,1)} %get-tuple-element.18.x_ref, bf16[2048,4096]{1,0:T(8,128)(2,1)} %w_ref.3, bf16[1,2048]{1,0:T(2,128)(2,1)} %reshape.43.g_ref, bf16[1,128]{1,0:T(2,128)(2,1)} %bitcast.27, f32[704,128]{1,0:T(8,128)} %get-tuple-element.32.cos_ref, ...), custom_call_target="tpu_custom_call" | custom-call | flops 51539607552 | bytes 37748736 | tf_op jit(solution)/shard_map/q_proj/pallas_call | solution.py:155
  125.8 0.7 dynamic_slice.6.given_ref
  126.4 6.5 reshape.46
  132.9 2.9 reshape.47
  135.8 23.4 %attn.4.after_ref.refs_0_ = bf16[1,512,4096]{2,1,0:T(8,128)(2,1)} custom-call(s32[197]{0:T(256)} %bitcast.8, bf16[6,512,4096]{2,1,0:T(8,128)(2,1)} %q_proj.2.refs_0_, bf16[8,1,2,512,512]{4,3,2,1,0:T(8,128)(2,1)} %bitcast.22, bf16[8,1,2,512,512]{4,3,2,1,0:T(8,128)(2,1)} %bitcast.23, s32[197]{0:T(256)} %bitcast.9), custom_call_target="tpu_custom_call" | custom-call | flops 34359738368 | bytes 8388608 | tf_op jit(solution)/shard_map/attn/pallas_call | solution.py:334
  159.3 84.0 %collective-permute-done.x_ref.refs_3_.refs_2_ = bf16[6,192,2048]{2,1,0:T(8,128)(2,1)} collective-permute-done((bf16[6,192,2048]{2,1,0:T(8,128)(2,1)}, bf16[6,192,2048]{2,1,0:T(8,128)(2,1)}, u32[]{:S(2)}, u32[]{:S(2)}) %collective-permute-start) | collective-permute-done | bytes 4718624 | tf_op jit(solution)/shard_map/ppermute | solution.py:514
  243.3 32.8 %q_proj.3.refs_0_.refs_1_ = bf16[6,192,4096]{2,1,0:T(8,128)(2,1)} custom-call(s32[197]{0:T(256)} %bitcast.10, bf16[6,192,2048]{2,1,0:T(8,128)(2,1)} %collective-permute-done.x_ref.refs_3_.refs_2_, bf16[2048,4096]{1,0:T(8,128)(2,1)} %w_ref.3, bf16[1,2048]{1,0:T(2,128)(2,1)} %reshape.43.g_ref, bf16[1,128]{1,0:T(2,128)(2,1)} %bitcast.28, ...), custom_call_target="tpu_custom_call" | custom-call | flops 19327352832 | bytes 14155776 | tf_op jit(solution)/shard_map/q_proj/pallas_call | solution.py:155
  276.1 36.9 %attn.5.refs_4_.refs_0_ = bf16[1,192,4096]{2,1,0:T(8,128)(2,1)} custom-call(s32[197]{0:T(256)} %bitcast.11, bf16[6,192,4096]{2,1,0:T(8,128)(2,1)} %q_proj.3.refs_0_.refs_1_, bf16[8,1,2,512,512]{4,3,2,1,0:T(8,128)(2,1)} %bitcast.24, bf16[8,1,2,512,512]{4,3,2,1,0:T(8,128)(2,1)} %bitcast.25, s32[197]{0:T(256)} %bitcast.12), custom_call_target="tpu_custom_call" | custom-call | flops 12884901888 | bytes 3145728 | tf_op jit(solution)/shard_map/attn/pallas_call | solution.py:334
  313.1 100.8 %attn.6 = (bf16[2,512,4096]{2,1,0:T(8,128)(2,1)}, bf16[2,192,4096]{2,1,0:T(8,128)(2,1)}) custom-call(s32[197]{0:T(256)} %bitcast.13, bf16[6,512,4096]{2,1,0:T(8,128)(2,1)} %q_proj.2.refs_0_, bf16[6,192,4096]{2,1,0:T(8,128)(2,1)} %q_proj.3.refs_0_.refs_1_, bf16[8,2,2,512,512]{4,3,2,1,0:T(8,128)(2,1)} %bitcast.20, bf16[8,2,2,512,512]{4,3,2,1,0:T(8,128)(2,1)} %bitcast.21, ...), custom_call_target="tpu_custom_call" | custom-call | flops 94489280512 | bytes 23068672 | tf_op jit(solution)/shard_map/attn/pallas_call | solution.py:334
  413.8 15.9 %out_moved.2.refs_4_ = bf16[3,192,2048]{2,1,0:T(8,128)(2,1)} custom-call(s32[197]{0:T(256)} %bitcast.14, bf16[1,192,4096]{2,1,0:T(8,128)(2,1)} %attn.5.refs_4_.refs_0_, bf16[2,192,4096]{2,1,0:T(8,128)(2,1)} %get-tuple-element.22.refs_1_, bf16[4096,2048]{1,0:T(8,128)(2,1)} %refs_3_.1, bf16[6,192,2048]{2,1,0:T(8,128)(2,1)} %collective-permute-done.x_ref.refs_3_.refs_2_), custom_call_target="tpu_custom_call" | custom-call | flops 9663676416 | bytes 16777216 | tf_op jit(solution)/shard_map/out_moved/pallas_call | solution.py:379
  429.8 3.0 collective-permute-start.1
  432.8 146.2 %attn.7 = (bf16[3,512,4096]{2,1,0:T(8,128)(2,1)}, bf16[3,192,4096]{2,1,0:T(8,128)(2,1)}) custom-call(s32[197]{0:T(256)} %bitcast.15, bf16[6,512,4096]{2,1,0:T(8,128)(2,1)} %q_proj.2.refs_0_, bf16[6,192,4096]{2,1,0:T(8,128)(2,1)} %q_proj.3.refs_0_.refs_1_, bf16[8,3,2,512,512]{4,3,2,1,0:T(8,128)(2,1)} %bitcast.18, bf16[8,3,2,512,512]{4,3,2,1,0:T(8,128)(2,1)} %bitcast.19, ...), custom_call_target="tpu_custom_call" | custom-call | flops 141733920768 | bytes 34603008 | tf_op jit(solution)/shard_map/attn/pallas_call | solution.py:334
  579.0 15.9 %out_moved.3.refs_5_ = bf16[3,192,2048]{2,1,0:T(8,128)(2,1)} custom-call(s32[197]{0:T(256)} %bitcast.16, bf16[3,192,4096]{2,1,0:T(8,128)(2,1)} %get-tuple-element.24.refs_0_, bf16[4096,2048]{1,0:T(8,128)(2,1)} %refs_3_.1, bf16[6,192,2048]{2,1,0:T(8,128)(2,1)} %collective-permute-done.x_ref.refs_3_.refs_2_), custom_call_target="tpu_custom_call" | custom-call | flops 9663676416 | bytes 16777216 | tf_op jit(solution)/shard_map/out_moved/pallas_call | solution.py:379
  594.9 1.7 collective-permute-start.2
  596.6 64.5 %out_local.1.refs_2_ = bf16[6,512,2048]{2,1,0:T(8,128)(2,1)} custom-call(s32[197]{0:T(256)} %bitcast.17, bf16[1,512,4096]{2,1,0:T(8,128)(2,1)} %attn.4.after_ref.refs_0_, bf16[2,512,4096]{2,1,0:T(8,128)(2,1)} %get-tuple-element.25.refs_1_, bf16[3,512,4096]{2,1,0:T(8,128)(2,1)} %get-tuple-element.26.refs_2_, bf16[4096,2048]{1,0:T(8,128)(2,1)} %refs_3_.1, ...), custom_call_target="tpu_custom_call" | custom-call | flops 51539607552 | bytes 37748736 | tf_op jit(solution)/shard_map/out_local/pallas_call | solution.py:434
  661.2 1.4 copy-done.1
  662.6 4.2 merge.1
  (14 shorter events, 0.1 us)
Async XLA Ops:
  7.2 128.7 %all-gather.7.cloned.1.call-start = ((), (), s32[]{:S(2)}) async-start(), calls=%async_computation | async-start | bytes 9437184 | tf_op jit(solution)/shard_map/all_gather | solution.py:525
  40.6 272.5 %all-gather.9.cloned.1.call-start = ((), (), s32[]{:S(2)}) async-start(), calls=%async_computation.1 | async-start | bytes 18874368 | tf_op jit(solution)/shard_map/all_gather | solution.py:525
  41.4 391.3 %all-gather.11.cloned.1.call-start = ((), (), s32[]{:S(2)}) async-start(), calls=%async_computation.2 | async-start | bytes 28311552 | tf_op jit(solution)/shard_map/all_gather | solution.py:525
  47.4 195.9 %collective-permute-start = (bf16[6,192,2048]{2,1,0:T(8,128)(2,1)}, bf16[6,192,2048]{2,1,0:T(8,128)(2,1)}, u32[]{:S(2)}, u32[]{:S(2)}) collective-permute-start(bf16[6,192,2048]{2,1,0:T(8,128)(2,1)} %slice.3), channel_id=1, source_target_pairs={{5,2},{6,1},{7,0},{13,10},{14,9},{15,8}} | collective-permute-start | bytes 14155784 | tf_op jit(solution)/shard_map/ppermute | solution.py:514
  50.0 75.8 %copy-start.2 = (s32[8]{0:T(128)S(1)}, s32[8]{0:T(128)}, u32[]{:S(2)}) copy-start(s32[8]{0:T(128)} %constant.28.clone) | copy-start | bytes 100
  125.8 7.1 %copy-start = (bf16[6,512,512]{2,1,0:T(8,128)(2,1)S(1)}, bf16[6,512,512]{2,1,0:T(8,128)(2,1)}, u32[]{:S(2)}) copy-start(bf16[6,512,512]{2,1,0:T(8,128)(2,1)} %get-tuple-element.28) | copy-start | bytes 9437188
  429.8 231.4 %collective-permute-start.1 = (bf16[3,192,2048]{2,1,0:T(8,128)(2,1)}, bf16[3,192,2048]{2,1,0:T(8,128)(2,1)}, u32[]{:S(2)}, u32[]{:S(2)}) collective-permute-start(bf16[3,192,2048]{2,1,0:T(8,128)(2,1)} %out_moved.2.refs_4_), channel_id=1, source_target_pairs={{2,5},{1,6},{0,7},{10,13},{9,14},{8,15}} | collective-permute-start | bytes 7077896 | tf_op jit(solution)/shard_map/ppermute | solution.py:542
  594.9 66.3 %collective-permute-start.2 = (bf16[3,192,2048]{2,1,0:T(8,128)(2,1)}, bf16[3,192,2048]{2,1,0:T(8,128)(2,1)S(1)}, u32[]{:S(2)}, u32[]{:S(2)}) collective-permute-start(bf16[3,192,2048]{2,1,0:T(8,128)(2,1)} %out_moved.3.refs_5_), channel_id=1, source_target_pairs={{2,5},{1,6},{0,7},{10,13},{9,14},{8,15}} | collective-permute-start | bytes 7077896 | tf_op jit(solution)/shard_map/ppermute | solution.py:542
  661.2 1.4 copy-start.1
Sparse Core Ops, SparseCore 0:
  40.7 82.2 all-gather.6
  124.7 133.4 all-gather.8
  259.7 114.9 all-gather.10

commit v3 on v2

--- a/solution.py
+++ b/solution.py
@@ -47,7 +47,8 @@
     return (y * cos[None] + rolled * sin[None]).astype(jnp.bfloat16)
 
 
-def kv_kernel(sizes, x_ref, wk_ref, wv_ref, g_ref, kg_ref, cos_ref, sin_ref, k_ref, v_ref, h_ref, *pack_refs):
+def kv_kernel(sizes, x_ref, wk_ref, wv_ref, g_ref, kg_ref, cos_ref, sin_ref, *rest):
+    k_ref, v_ref, h_ref, *pack_refs = rest[-3 - len(sizes):]
     n_p, r, d = x_ref.shape
     i = pl.program_id(0)
     h = normed(x_ref, g_ref)
@@ -73,12 +74,13 @@
             at += size
 
 
-def kv_project(x, w_key, w_value, gain, k_gain, cos, sin, sizes):
+def kv_project(x, w_key, w_value, gain, k_gain, cos, sin, sizes, first, into):
     n_p, rows, d = x.shape
     w = w_key.shape[1]
-    r = min(128, rows)
+    n = sum(sizes)
+    r = rows if n == 1 else min(128, rows)
     whole = lambda shape: pl.BlockSpec(shape, lambda i: (0,) * len(shape))
-    cut = lambda cols: pl.BlockSpec((n_p, r, cols), lambda i: (0, i, 0))
+    cut = lambda cols: pl.BlockSpec((pl.Element(n), pl.Element(r), pl.Element(cols)), lambda i: (first, i * r, 0))
     packs = [(s, 2, rows, w) for s in sizes]
     return pl.pallas_call(
         functools.partial(kv_kernel, sizes),
@@ -87,12 +89,13 @@
         in_specs=[
             cut(d), whole((d, w)), whole((d, w)), whole((1, d)), whole((1, HD)),
             pl.BlockSpec((r, HD), lambda i: (i, 0)), pl.BlockSpec((r, HD), lambda i: (i, 0)),
-        ],
+        ] + [pl.BlockSpec(memory_space=pl.ANY)] * len(into),
         out_specs=[cut(w), cut(w), cut(d)] + [whole(s) for s in packs],
+        input_output_aliases={7 + i: i for i in range(len(into))},
         compiler_params=pltpu.CompilerParams(dimension_semantics=("arbitrary",), vmem_limit_bytes=VMEM_LIMIT),
-        cost_estimate=pl.CostEstimate(flops=4 * n_p * rows * d * w, bytes_accessed=8 * n_p * rows * d, transcendentals=0),
+        cost_estimate=pl.CostEstimate(flops=4 * n * rows * d * w, bytes_accessed=8 * n * rows * d, transcendentals=0),
         name="kv_proj",
-    )(x, w_key, w_value, gain, k_gain, cos, sin)
+    )(x, w_key, w_value, gain, k_gain, cos, sin, *into)
 
 
 def q_kernel(nc, is_normed, step_of, info_ref, x_ref, w_ref, g_ref, qg_ref, cos_ref, sin_ref, after_ref, q_ref, h_scr, y_scr, w_scr, sem):
@@ -129,7 +132,7 @@
         def finish(n):
             for j in range(nc // HD):
                 y = head_norm_rope(y_scr[:, j * HD:(j + 1) * HD].astype(jnp.float32), gain, cos, sin, n_p)
-                q_ref[:, :, pl.ds(pl.multiple_of(n * nc + j * HD, HD), HD)] = y
+                q_ref[:, 0, n * (nc // HD) + j] = y
 
         def step(n, _):
             arrived(n + 1)
@@ -154,7 +157,7 @@
     nc = Q_COLS
     return pl.pallas_call(
         functools.partial(q_kernel, nc, is_normed, lambda info: (begin(info), first_tile)),
-        out_shape=jax.ShapeDtypeStruct((n_p, rows, w), x.dtype),
+        out_shape=jax.ShapeDtypeStruct((n_p, n_tiles, w // HD, T, HD), x.dtype),
         grid_spec=pltpu.PrefetchScalarGridSpec(
             num_scalar_prefetch=1,
             grid=(n_tiles,),
@@ -164,7 +167,7 @@
                 whole((1, d)), whole((1, HD)), table, table,
                 pl.BlockSpec(memory_space=pl.ANY),
             ],
-            out_specs=pl.BlockSpec((n_p, T, w), lambda i, info: (0, local(i, info), 0)),
+            out_specs=pl.BlockSpec((n_p, 1, w // HD, T, HD), lambda i, info: (0, local(i, info), 0, 0, 0)),
             scratch_shapes=[
                 pltpu.VMEM((n_p * T, d), x.dtype), pltpu.VMEM((n_p * T, nc), x.dtype),
                 pltpu.VMEM((d, w), x.dtype), pltpu.SemaphoreType.DMA((w // nc,)),
@@ -179,7 +182,7 @@
 def attn_kernel(n_tiles, parts, grp, bk, ext_step, hp, ck, info_ref, *refs):
     n_q = len(parts)
     q_refs, (k_ref, v_ref, _), o_refs = refs[:n_q], refs[n_q:n_q + 3], refs[n_q + 3:2 * n_q + 3]
-    q_scr, s_scr, bm_scr, m_scr, l_scr, acc_scr = refs[2 * n_q + 3:]
+    s_scr, bm_scr, m_scr, l_scr, acc_scr, *q_scr = refs[2 * n_q + 3:]
     first_tile = parts[0][0]
     n = grp * T
     base = 2 * n_tiles + 3
@@ -199,17 +202,22 @@
         acc_scr[...] = jnp.zeros_like(acc_scr)
         m_scr[...] = jnp.zeros_like(m_scr)
 
-    for h in range(hp):
-        for (start, tiles), q_ref in zip(parts, q_refs):
-            for t in range(tiles):
-                for j in range(grp):
-                    q_scr[h, start - first_tile + t, j * T:(j + 1) * T, :] = q_ref[0, t * T:(t + 1) * T, (h * grp + j) * HD:(h * grp + j + 1) * HD]
+    if n_q > 1:
+        at = 0
+        for (_, tiles), q_ref in zip(parts, q_refs):
+            q_scr[0][at:at + tiles] = q_ref[0]
+            at += tiles
+
+    def q_rows(t, h):
+        t = jnp.clip(t - first_tile, 0, sum(tiles for _, tiles in parts) - 1)
+        src = q_scr[0].at[t] if n_q > 1 else q_refs[0].at[0, t]
+        return src[h * grp:(h + 1) * grp].reshape(n, HD)
 
     def fold(x, op):
         return op(x.reshape(x.shape[0] // 8, 8, n), axis=0)
 
     def qk_chunk(i, h, r):
-        s = lax.dot_general(k_ref[blk(i), r * ck:(r + 1) * ck, h * HD:(h + 1) * HD], q_scr[h, jnp.clip(tile(i) - first_tile, 0, q_scr.shape[1] - 1)], (((1,), (1,)), ((), ())), preferred_element_type=jnp.float32)
+        s = lax.dot_general(k_ref[blk(i), r * ck:(r + 1) * ck, h * HD:(h + 1) * HD], q_rows(tile(i), h), (((1,), (1,)), ((), ())), preferred_element_type=jnp.float32)
         s_scr[h, r * ck:(r + 1) * ck, :] = s
         return fold(s, jnp.max)
 
@@ -324,36 +332,36 @@
 
 
 def attention(qs, firsts, kv, info, after, first_prompt, n_kv, total_tiles, hp=4, ck=256):
-    width = qs[0].shape[2]
-    grp = width // HD // n_kv
+    heads = qs[0].shape[2]
+    grp = heads // n_kv
     n_dev, nb, _, bk, _ = kv.shape
-    parts = [(f, q.shape[1] // T) for f, q in zip(firsts, qs)]
+    parts = [(f, q.shape[1]) for f, q in zip(firsts, qs)]
     n_tiles = sum(t for _, t in parts)
     n = grp * T
-    flops = 2 * 4 * nb * n_tiles * T * width * n_dev * bk // 2
+    flops = 2 * 4 * nb * n_tiles * T * heads * HD * n_dev * bk // 2
+    hh = hp * grp
     return pl.pallas_call(
         functools.partial(attn_kernel, total_tiles, parts, grp, bk, DIAG_STEP, hp, ck),
-        out_shape=[jax.ShapeDtypeStruct((nb,) + q.shape[1:], q.dtype) for q in qs],
+        out_shape=[jax.ShapeDtypeStruct((nb, t * T, heads * HD), qs[0].dtype) for _, t in parts],
         grid_spec=pltpu.PrefetchScalarGridSpec(
             num_scalar_prefetch=1,
             grid=(nb, n_kv // hp),
-            in_specs=[pl.BlockSpec((1, q.shape[1], hp * grp * HD), lambda p, h, *_: (p + first_prompt, 0, h)) for q in qs] + [
+            in_specs=[pl.BlockSpec((1, t, hh, T, HD), lambda p, h, *_: (p + first_prompt, 0, h, 0, 0)) for _, t in parts] + [
                 pl.BlockSpec((n_dev, None, None, bk, hp * HD), lambda p, h, *_: (0, p, 0, 0, h)),
                 pl.BlockSpec((n_dev, None, None, hp * HD, bk), lambda p, h, *_: (0, p, 1, h, 0)),
                 pl.BlockSpec(memory_space=pl.ANY),
             ],
-            out_specs=[pl.BlockSpec((1, q.shape[1], hp * grp * HD), lambda p, h, *_: (p, 0, h)) for q in qs],
+            out_specs=[pl.BlockSpec((1, t * T, hh * HD), lambda p, h, *_: (p, 0, h)) for _, t in parts],
             scratch_shapes=[
-                pltpu.VMEM((hp, n_tiles, n, HD), qs[0].dtype),
                 pltpu.VMEM((hp, bk, n), jnp.float32),
                 pltpu.VMEM((hp, 8, n), jnp.float32),
                 pltpu.VMEM((hp, 1, n), jnp.float32),
                 pltpu.VMEM((hp, 8, n), jnp.float32),
                 pltpu.VMEM((hp, HD, n), jnp.float32),
-            ],
+            ] + ([pltpu.VMEM((n_tiles, hh, T, HD), qs[0].dtype)] if len(qs) > 1 else []),
         ),
         compiler_params=pltpu.CompilerParams(dimension_semantics=("arbitrary", "arbitrary"), vmem_limit_bytes=VMEM_LIMIT),
-        cost_estimate=pl.CostEstimate(flops=flops, bytes_accessed=4 * nb * n_tiles * T * width, transcendentals=0),
+        cost_estimate=pl.CostEstimate(flops=flops, bytes_accessed=4 * nb * n_tiles * T * heads * HD, transcendentals=0),
         name="attn",
     )(info, *qs, kv, kv, after)
 
@@ -504,7 +512,7 @@
         n_tiles = seq_loc // T
         sizes = []
         while sum(sizes) < n_p:
-            sizes.append(min(len(sizes) + 1, n_p - sum(sizes)))
+            sizes.append(min(len(sizes) + 1, 2, n_p - sum(sizes)))
         table = split_work(n_sp, n_tiles)
         spare = max(table)
         me = lax.axis_index("sp")
@@ -521,7 +529,13 @@
         info = jnp.asarray(make_info(n_sp, seq_loc, table, DIAG_STEP))[me]
 
         given = jnp.asarray(table, jnp.int32)[me].reshape(1)
-        k, v, h, *packs = kv_project(tokens, w_key, w_value, gain, k_gain, cos, sin, sizes)
+        *into, pack = kv_project(tokens, w_key, w_value, gain, k_gain, cos, sin, sizes[:1], 0, ())
+        packs = [pack]
+        if sizes[1:]:
+            k, v, h, *more = kv_project(tokens, w_key, w_value, gain, k_gain, cos, sin, sizes[1:], sizes[0], into)
+            packs += more
+        else:
+            k, v, h = into
         kv = [lax.all_gather(pack, "sp") for pack in packs]
         total = n_tiles + spare
         q = q_project(h, w_query, gain, q_gain, cos, sin, info, 0, total, True, info)
@@ -538,9 +552,11 @@
             at += sizes[g]
             own.append(o)
             extra.append(o_x)
-            after = out_moved(extra, w_out, x_moved, info, done, total)
-            returned.append(lax.ppermute(after, "sp", [(b, a) for a, b in away]))
-            done, extra = at, []
+            after = o_x
+            if 2 * (at - done) >= n_p or g == len(sizes) - 1:
+                after = out_moved(extra, w_out, x_moved, info, done, total)
+                returned.append(lax.ppermute(after, "sp", [(b, a) for a, b in away]))
+                done, extra = at, []
         out = out_local(own, w_out, tokens, info, after)
         out = merge(returned, out, given)
         return out, k.reshape(n_p, seq_loc, n_kv, HD), v.reshape(n_p, seq_loc, n_kv, HD)

time: 682 us -> 680 us (level)
  waiting for transfers between devices: 85.6 us -> 75.2 us
  Pallas kernels: 546 us -> 556 us
    ppermute x1, waiting for transfers between devices: 84 us -> 74.3 us  [block(): x_moved = lax.ppermute(tokens[:, seq_loc - spare * T:, :], 'sp', away)]
    pallas_call x4 -> x5, Pallas kernels: 307 us -> 314 us  [attention(): pl.pallas_call(functools.partial(attn_kernel, total_tiles, parts, grp, bk...]
    pallas_call x1 -> x2, Pallas kernels: 29.3 us -> 32.1 us  [kv_project(): pl.pallas_call(functools.partial(kv_kernel, sizes), out_shape=[jax.ShapeD...]
  transfers between devices with their start and end apart: 6 -> 7, of which waited for: 1 -> 1; matrix products, arithmetic and copies ran while one was open for 2% -> 2% of each run, Pallas kernels for 76% -> 81%
where the time goes in v3:
time: 680 us; the launch traced here: 672 us
  Pallas kernels  556 us (82%)
  waiting for transfers between devices  75.2 us (11%)
  local copies, waits for them, and re-layouts  18.4 us (3%)
  between operations  14.1 us (2%)
    pallas_call x5, Pallas kernels, attention(): pl.pallas_call(functools.partial(attn_kernel, total_tiles, parts, grp, bk...  314 us
    pallas_call x2, Pallas kernels, q_project(): pl.pallas_call(functools.partial(q_kernel, nc, is_normed, lambda info: (b...  109 us
    ppermute x1, waiting for transfers between devices, block(): x_moved = lax.ppermute(tokens[:, seq_loc - spare * T:, :], 'sp', away)  74.3 us
    pallas_call x1, Pallas kernels, out_local(): pl.pallas_call(functools.partial(out_kernel, n_g, nc), out_shape=jax.Shap...  64.5 us
    pallas_call x2, Pallas kernels, kv_project(): pl.pallas_call(functools.partial(kv_kernel, sizes), out_shape=[jax.ShapeD...  32.1 us
    pallas_call x2, Pallas kernels, out_moved(): pl.pallas_call(functools.partial(out_moved_kernel, taken, len(o_parts)),...  31.8 us
  transfers between devices with their start and end apart: 7, of which 1 were waited for; matrix products, arithmetic and copies ran while one was open for 2% of the time, Pallas kernels for 81%

profile of v3, /device:TPU:112, one launch (start us, length us, event | category | flops | bytes accessed | tf_op | source)
XLA Modules:
  0.0 672.3 jit_solution(13429724153087235541)
XLA Ops:
  7.3 0.1 pad_add_fusion
  7.4 0.1 add_convert_fusion
  7.4 0.1 convert_element_type.11
  7.5 1.3 reshape.43.g_ref
  8.8 1.3 fusion
  10.1 1.1 pad_maximum_fusion
  11.3 7.8 %kv_proj.2 = (bf16[6,512,512]{2,1,0:T(8,128)(2,1)}, bf16[6,512,512]{2,1,0:T(8,128)(2,1)}, bf16[6,512,2048]{2,1,0:T(8,128)(2,1)}, bf16[1,2,512,512]{3,2,1,0:T(8,128)(2,1)}) custom-call(bf16[6,512,2048]{2,1,0:T(8,128)(2,1)} %refs_5_.1, bf16[2048,512]{1,0:T(8,128)(2,1)} %wk_ref.3, bf16[2048,512]{1,0:T(8,128)(2,1)} %wv_ref.3, bf16[1,2048]{1,0:T(2,128)(2,1)} %reshape.43.g_ref, ...), custom_call_target="tpu_custom_call" | custom-call | flops 2147483648 | bytes 8388608 | tf_op jit(solution)/shard_map/kv_proj/pallas_call | solution.py:85
  19.2 0.1 all-gather.11.cloned.1.call-start
  19.2 24.3 %kv_proj.3 = (bf16[6,512,512]{2,1,0:T(8,128)(2,1)}, bf16[6,512,512]{2,1,0:T(8,128)(2,1)}, bf16[6,512,2048]{2,1,0:T(8,128)(2,1)}, bf16[2,2,512,512]{3,2,1,0:T(8,1...) custom-call(bf16[6,512,2048]{2,1,0:T(8,128)(2,1)} %refs_5_.1, ...), custom_call_target="tpu_custom_call", output_to_operand_aliasing={{0}: (7, {}), {1}: (8, {}), {2}: (9, {})} | custom-call | flops 10737418240 | bytes 41943040 | tf_op jit(solution)/shard_map/kv_proj/pallas_call | solution.py:85
  43.6 0.1 all-gather.13.cloned.1.call-start
  43.6 0.7 all-gather.13.cloned.1.call-update
  44.4 5.3 slice.3
  49.7 1.5 collective-permute-start
  51.3 1.2 constant_dynamic-slice_fusion
  52.5 76.2 %q_proj.2.refs_0_ = bf16[6,8,32,64,128]{4,3,2,1,0:T(8,128)(2,1)} custom-call(s32[197]{0:T(256)} %bitcast.7, bf16[6,512,2048]{2,1,0:T(8,128)(2,1)} %get-tuple-element.27.x_ref, bf16[2048,4096]{1,0:T(8,128)(2,1)} %w_ref.3, bf16[1,2048]{1,0:T(2,128)(2,1)} %reshape.43.g_ref, bf16[1,128]{1,0:T(2,128)(2,1)} %bitcast.32, f32[704,128]{1,0:T(8,128)} %get-tuple-element.44.cos_ref, ...), custom_call_target="tpu_custom_call" | custom-call | flops 51539607552 | bytes 37748736 | tf_op jit(solution)/shard_map/q_proj/pallas_call | solution.py:158
  128.8 0.6 dynamic_slice.6.given_ref
  129.4 2.9 reshape.46
  132.3 5.5 reshape.47
  137.8 22.3 %attn.5.after_ref.refs_0_ = bf16[1,512,4096]{2,1,0:T(8,128)(2,1)} custom-call(s32[197]{0:T(256)} %bitcast.9, bf16[6,8,32,64,128]{4,3,2,1,0:T(8,128)(2,1)} %q_proj.2.refs_0_, bf16[8,1,2,512,512]{4,3,2,1,0:T(8,128)(2,1)} %bitcast.26, bf16[8,1,2,512,512]{4,3,2,1,0:T(8,128)(2,1)} %bitcast.27, s32[197]{0:T(256)} %bitcast.10), custom_call_target="tpu_custom_call" | custom-call | flops 34359738368 | bytes 8388608 | tf_op jit(solution)/shard_map/attn/pallas_call | solution.py:343
  160.2 74.3 %collective-permute-done.x_ref.refs_3_ = bf16[6,192,2048]{2,1,0:T(8,128)(2,1)} collective-permute-done((bf16[6,192,2048]{2,1,0:T(8,128)(2,1)}, bf16[6,192,2048]{2,1,0:T(8,128)(2,1)}, u32[]{:S(2)}, u32[]{:S(2)}) %collective-permute-start) | collective-permute-done | bytes 4718624 | tf_op jit(solution)/shard_map/ppermute | solution.py:522
  234.4 33.0 %q_proj.3.refs_0_.refs_1_ = bf16[6,3,32,64,128]{4,3,2,1,0:T(8,128)(2,1)} custom-call(s32[197]{0:T(256)} %bitcast.11, bf16[6,192,2048]{2,1,0:T(8,128)(2,1)} %collective-permute-done.x_ref.refs_3_, bf16[2048,4096]{1,0:T(8,128)(2,1)} %w_ref.3, bf16[1,2048]{1,0:T(2,128)(2,1)} %reshape.43.g_ref, bf16[1,128]{1,0:T(2,128)(2,1)} %bitcast.33, ...), custom_call_target="tpu_custom_call" | custom-call | flops 19327352832 | bytes 14155776 | tf_op jit(solution)/shard_map/q_proj/pallas_call | solution.py:158
  267.5 36.9 %attn.6.refs_4_.refs_0_ = bf16[1,192,4096]{2,1,0:T(8,128)(2,1)} custom-call(s32[197]{0:T(256)} %bitcast.12, bf16[6,3,32,64,128]{4,3,2,1,0:T(8,128)(2,1)} %q_proj.3.refs_0_.refs_1_, bf16[8,1,2,512,512]{4,3,2,1,0:T(8,128)(2,1)} %bitcast.28, bf16[8,1,2,512,512]{4,3,2,1,0:T(8,128)(2,1)} %bitcast.29, s32[197]{0:T(256)} %bitcast.13), custom_call_target="tpu_custom_call" | custom-call | flops 12884901888 | bytes 3145728 | tf_op jit(solution)/shard_map/attn/pallas_call | solution.py:343
  304.4 100.1 %attn.7 = (bf16[2,512,4096]{2,1,0:T(8,128)(2,1)}, bf16[2,192,4096]{2,1,0:T(8,128)(2,1)}) custom-call(s32[197]{0:T(256)} %bitcast.14, bf16[6,8,32,64,128]{4,3,2,1,0:T(8,128)(2,1)} %q_proj.2.refs_0_, bf16[6,3,32,64,128]{4,3,2,1,0:T(8,128)(2,1)} %q_proj.3.refs_0_.refs_1_, bf16[8,2,2,512,512]{4,3,2,1,0:T(8,128)(2,1)} %bitcast.24, ...), custom_call_target="tpu_custom_call" | custom-call | flops 94489280512 | bytes 23068672 | tf_op jit(solution)/shard_map/attn/pallas_call | solution.py:343
  404.5 15.9 %out_moved.2.refs_4_ = bf16[3,192,2048]{2,1,0:T(8,128)(2,1)} custom-call(s32[197]{0:T(256)} %bitcast.15, bf16[1,192,4096]{2,1,0:T(8,128)(2,1)} %attn.6.refs_4_.refs_0_, bf16[2,192,4096]{2,1,0:T(8,128)(2,1)} %get-tuple-element.31.refs_1_, bf16[4096,2048]{1,0:T(8,128)(2,1)} %refs_4_.1, bf16[6,192,2048]{2,1,0:T(8,128)(2,1)} %collective-permute-done.x_ref.refs_3_), custom_call_target="tpu_custom_call" | custom-call | flops 9663676416 | bytes 16777216 | tf_op jit(solution)/shard_map/out_moved/pallas_call | solution.py:387
  420.4 3.1 collective-permute-start.1
  423.5 100.1 %attn.8 = (bf16[2,512,4096]{2,1,0:T(8,128)(2,1)}, bf16[2,192,4096]{2,1,0:T(8,128)(2,1)}) custom-call(s32[197]{0:T(256)} %bitcast.16, bf16[6,8,32,64,128]{4,3,2,1,0:T(8,128)(2,1)} %q_proj.2.refs_0_, bf16[6,3,32,64,128]{4,3,2,1,0:T(8,128)(2,1)} %q_proj.3.refs_0_.refs_1_, bf16[8,2,2,512,512]{4,3,2,1,0:T(8,128)(2,1)} %bitcast.22, ...), custom_call_target="tpu_custom_call" | custom-call | flops 94489280512 | bytes 23068672 | tf_op jit(solution)/shard_map/attn/pallas_call | solution.py:343
  523.6 54.4 %attn.9 = (bf16[1,512,4096]{2,1,0:T(8,128)(2,1)}, bf16[1,192,4096]{2,1,0:T(8,128)(2,1)}) custom-call(s32[197]{0:T(256)} %bitcast.17, bf16[6,8,32,64,128]{4,3,2,1,0:T(8,128)(2,1)} %q_proj.2.refs_0_, bf16[6,3,32,64,128]{4,3,2,1,0:T(8,128)(2,1)} %q_proj.3.refs_0_.refs_1_, bf16[8,1,2,512,512]{4,3,2,1,0:T(8,128)(2,1)} %bitcast.30, ...), custom_call_target="tpu_custom_call" | custom-call | flops 47244640256 | bytes 11534336 | tf_op jit(solution)/shard_map/attn/pallas_call | solution.py:343
  578.0 15.9 %out_moved.3.refs_6_ = bf16[3,192,2048]{2,1,0:T(8,128)(2,1)} custom-call(s32[197]{0:T(256)} %bitcast.18, bf16[2,192,4096]{2,1,0:T(8,128)(2,1)} %get-tuple-element.33.refs_4_.refs_0_, bf16[1,192,4096]{2,1,0:T(8,128)(2,1)} %get-tuple-element.35.refs_1_, bf16[4096,2048]{1,0:T(8,128)(2,1)} %refs_4_.1, bf16[6,192,2048]{2,1,0:T(8,128)(2,1)} %collective-permute-done.x_ref.refs_3_), custom_call_target="tpu_custom_call" | custom-call | flops 9663676416 | bytes 16777216 | tf_op jit(solution)/shard_map/out_moved/pallas_call | solution.py:387
  593.9 1.4 collective-permute-start.2
  595.4 64.5 %out_local.1.refs_2_ = bf16[6,512,2048]{2,1,0:T(8,128)(2,1)} custom-call(s32[197]{0:T(256)} %bitcast.19, bf16[1,512,4096]{2,1,0:T(8,128)(2,1)} %attn.5.after_ref.refs_0_, bf16[2,512,4096]{2,1,0:T(8,128)(2,1)} %get-tuple-element.36.refs_1_, bf16[2,512,4096]{2,1,0:T(8,128)(2,1)} %get-tuple-element.37.refs_2_, bf16[1,512,4096]{2,1,0:T(8,128)(2,1)} %get-tuple-element.38.refs_3_, ...), custom_call_target="tpu_custom_call" | custom-call | flops 51539607552 | bytes 37748736 | tf_op jit(solution)/shard_map/out_local/pallas_call | solution.py:442
  660.0 1.4 copy-done.1
  661.4 4.2 merge.1
  (19 shorter events, 0.3 us)
Async XLA Ops:
  7.2 130.7 %all-gather.9.cloned.1.call-start = ((), (), s32[]{:S(2)}) async-start(), calls=%async_computation | async-start | bytes 9437184 | tf_op jit(solution)/shard_map/all_gather | solution.py:539
  19.2 285.2 %all-gather.11.cloned.1.call-start = ((), (), s32[]{:S(2)}) async-start(), calls=%async_computation.1 | async-start | bytes 18874368 | tf_op jit(solution)/shard_map/all_gather | solution.py:539
  43.6 379.9 %all-gather.13.cloned.1.call-start = ((), (), s32[]{:S(2)}) async-start(), calls=%async_computation.2 | async-start | bytes 18874368 | tf_op jit(solution)/shard_map/all_gather | solution.py:539
  44.4 479.2 %all-gather.15.cloned.1.call-start = ((), (), s32[]{:S(2)}) async-start(), calls=%async_computation.3 | async-start | bytes 9437184 | tf_op jit(solution)/shard_map/all_gather | solution.py:539
  49.7 184.7 %collective-permute-start = (bf16[6,192,2048]{2,1,0:T(8,128)(2,1)}, bf16[6,192,2048]{2,1,0:T(8,128)(2,1)}, u32[]{:S(2)}, u32[]{:S(2)}) collective-permute-start(bf16[6,192,2048]{2,1,0:T(8,128)(2,1)} %slice.3), channel_id=1, source_target_pairs={{5,2},{6,1},{7,0},{13,10},{14,9},{15,8}} | collective-permute-start | bytes 14155784 | tf_op jit(solution)/shard_map/ppermute | solution.py:522
  52.5 76.3 %copy-start.2 = (s32[8]{0:T(128)S(1)}, s32[8]{0:T(128)}, u32[]{:S(2)}) copy-start(s32[8]{0:T(128)} %constant.28.clone) | copy-start | bytes 100
  52.5 76.9 %copy-start = (bf16[6,512,512]{2,1,0:T(8,128)(2,1)S(1)}, bf16[6,512,512]{2,1,0:T(8,128)(2,1)}, u32[]{:S(2)}) copy-start(bf16[6,512,512]{2,1,0:T(8,128)(2,1)} %get-tuple-element.39) | copy-start | bytes 9437188
  420.4 239.5 %collective-permute-start.1 = (bf16[3,192,2048]{2,1,0:T(8,128)(2,1)}, bf16[3,192,2048]{2,1,0:T(8,128)(2,1)}, u32[]{:S(2)}, u32[]{:S(2)}) collective-permute-start(bf16[3,192,2048]{2,1,0:T(8,128)(2,1)} %out_moved.2.refs_4_), channel_id=1, source_target_pairs={{2,5},{1,6},{0,7},{10,13},{9,14},{8,15}} | collective-permute-start | bytes 7077896 | tf_op jit(solution)/shard_map/ppermute | solution.py:558
  593.9 66.0 %collective-permute-start.2 = (bf16[3,192,2048]{2,1,0:T(8,128)(2,1)}, bf16[3,192,2048]{2,1,0:T(8,128)(2,1)S(1)}, u32[]{:S(2)}, u32[]{:S(2)}) collective-permute-start(bf16[3,192,2048]{2,1,0:T(8,128)(2,1)} %out_moved.3.refs_6_), channel_id=1, source_target_pairs={{2,5},{1,6},{0,7},{10,13},{9,14},{8,15}} | collective-permute-start | bytes 7077896 | tf_op jit(solution)/shard_map/ppermute | solution.py:558
  660.0 1.4 copy-start.1
Sparse Core Ops, SparseCore 0:
  19.3 58.4 all-gather.8
  79.3 145.9 all-gather.10
  226.9 79.6 all-gather.12
  308.0 46.1 all-gather.14
